TPU v7x, 32 devices: a whole 2x2x4 slice. The times are simulated.
32 devices in a mesh: row: 8 (over y, x, core), col: 4 (over z).
Axes of the slice: x: 2, y: 2, z: 4, core: 2. Of those that a mesh axis runs over, the one named last changes fastest.
Arguments:
- columns: float32 [4096, 8192], P('col', 'row'), may hold values from -64 to 64
- block_order: int32 [64], P('col'), may hold values from 0 to 63, as said below
Outputs:
- rotated: float32 [4096, 8192], P('col', 'row')
Inputs may be any that keep to these rules, and one draw needn't show every extreme that they name: block_order is a permutation of 0 .. 63 in which slots c * 16 to (c + 1) * 16 - 1 name blocks c * 16 to (c + 1) * 16 - 1.
All inputs are finite; a program needn't handle non-finite values.
Results may differ from a plain program's by a relative error of at most 0.00055.
Values sent between devices are 32-bit elements; how exact they have to be, the bound alone decides.
A program may use at most 64 MiB of HBM per device.

v0:
```python
import functools

import jax
import jax.numpy as jnp
from jax import lax
from jax.experimental import pallas as pl
from jax.experimental.pallas import tpu as pltpu
from jax.sharding import PartitionSpec as P

BLOCK = 64
PAIR = 2 * BLOCK
STEPS = 4
HALF = BLOCK // 2
PACKED = HALF + 8
UPPER = 1.0 + BLOCK * BLOCK * 0.0905
HIGHEST = lax.Precision.HIGHEST


def split(a):
    high = a.astype(jnp.bfloat16)
    rest = a - high.astype(jnp.float32)
    middle = rest.astype(jnp.bfloat16)
    return high, middle, (rest - middle.astype(jnp.float32)).astype(jnp.bfloat16)


def chain(lefts, rights):
    return jnp.dot(
        jnp.concatenate(lefts, axis=1), jnp.concatenate(rights, axis=0), preferred_element_type=jnp.float32
    )


def mm3(a, b):
    (ah, am, _), (bh, bm, _) = split(a), split(b)
    return chain([ah, am, ah], [bh, bh, bm])


def mm4(a, b):
    (ah, am, al), (bh, bm, _) = split(a), split(b)
    return chain([al, am, ah, ah], [bh, bh, bm, bh])


def mm(a, b):
    (ah, am, al), (bh, bm, bl) = split(a), split(b)
    return chain([am, al, ah, ah, am, ah], [bm, bh, bl, bm, bh, bh])


def inverse(coupling, coupling_t, eye):
    system = eye + mm3(coupling, coupling_t)
    low = 2.0 / (1.0 + UPPER)
    y = system * low
    reach = low * (2.0 - low)
    scale = 2.0 / (1.0 + reach)
    z = 2.0 * eye - y
    x = (scale * low) * z
    y = scale * mm3(y, z)
    low = scale * reach
    while low < 0.99:
        z = 2.0 * eye - y
        reach = low * (2.0 - low)
        scale = 2.0 / (1.0 + reach)
        stacked = scale * mm3(jnp.concatenate([x, y], axis=0), z)
        x, y = stacked[:BLOCK], stacked[BLOCK:]
        low = scale * reach
    x = x + mm3(x, eye - mm3(system, x))
    product = mm(coupling_t, x)
    residual = eye - x - mm(coupling, product)
    stacked = jnp.concatenate([x, product], axis=0)
    stacked = stacked + mm3(stacked, residual)
    return stacked[:BLOCK], stacked[BLOCK:]


def turn_transposed(total):
    cross = jnp.concatenate([total[:HALF, :BLOCK], total[:HALF, BLOCK:]], axis=0)
    norms = total[HALF : HALF + 1, :]
    rows = lax.broadcasted_iota(jnp.int32, (BLOCK, BLOCK), 0)
    cols = lax.broadcasted_iota(jnp.int32, (BLOCK, BLOCK), 1)
    eye = jnp.where(rows == cols, 1.0, 0.0).astype(jnp.float32)
    top_norms = jnp.sum(jnp.where(rows == cols, norms[:, :BLOCK], 0.0), axis=1, keepdims=True)
    bottom_norms = norms[:, BLOCK:]
    spread = bottom_norms - top_norms
    square = spread * spread + 4.0 * cross * cross
    radius = jnp.sqrt(square)
    scale_term = (top_norms + bottom_norms) / BLOCK
    coupling = 2.0 * cross * spread / (square + jnp.abs(spread) * radius + scale_term * scale_term)
    coupling_t = coupling.T
    x, product = inverse(coupling, coupling_t, eye)
    lower = 2.0 * product
    corner = eye - mm(lower, coupling)
    diagonal = jnp.sum(jnp.where(rows == cols, corner, 0.0), axis=0, keepdims=True)
    mixed = jnp.where(rows <= cols, 2.0 * x - eye, corner)
    body = jnp.concatenate([mixed, -lower.T], axis=1)
    foot = jnp.broadcast_to(jnp.concatenate([diagonal, diagonal], axis=1), (8, PAIR))
    return jnp.concatenate([body, foot], axis=0)


def unpacked(packed):
    rows = lax.broadcasted_iota(jnp.int32, (BLOCK, BLOCK), 0)
    cols = lax.broadcasted_iota(jnp.int32, (BLOCK, BLOCK), 1)
    mixed, upper = packed[:BLOCK, :BLOCK], packed[:BLOCK, BLOCK:]
    flipped = mixed.T
    corner = jnp.where(rows == cols, packed[BLOCK : BLOCK + 1, :BLOCK], jnp.where(rows > cols, mixed, flipped))
    return jnp.concatenate(
        [
            jnp.concatenate([jnp.where(rows <= cols, mixed, flipped), upper], axis=1),
            jnp.concatenate([-upper.T, corner], axis=1),
        ],
        axis=0,
    )


def kernel(rows, cols, pairs, order_ref, columns_ref, out_ref, x, grams, parts, turns, edges,
           gram_send, gram_recv, turn_send, turn_recv, pass_send, edge_send, edge_recv, out_sem):
    me = lax.axis_index("row")
    position = lax.axis_index("col")
    core = lax.rem(me, 2)
    chip = lax.div(me, 2)
    partner = me + 1 - 2 * core
    has_left = position > 0
    has_right = position < cols - 1
    last = pairs - 1
    width = pairs * PAIR

    barrier = pltpu.get_barrier_semaphore()

    def greet(other, carry):
        @pl.when(other != me)
        def _():
            pl.semaphore_signal(barrier, inc=1, device_id={"row": other})
        return carry

    lax.fori_loop(0, rows, greet, 0)

    @pl.when(has_left)
    def _():
        pl.semaphore_signal(barrier, inc=1, device_id={"col": position - 1})

    @pl.when(has_right)
    def _():
        pl.semaphore_signal(barrier, inc=1, device_id={"col": position + 1})

    def fill(slot, carry):
        source = lax.rem(order_ref[slot], 2 * pairs)
        x[0, pl.ds(pl.multiple_of(slot * BLOCK, BLOCK), BLOCK), :] = columns_ref[source]
        return carry

    lax.fori_loop(0, 2 * pairs, fill, 0)

    greeted = rows - 1 + has_left.astype(jnp.int32) + has_right.astype(jnp.int32)
    pl.semaphore_wait(barrier, greeted)

    def gram_copy(pair):
        return pltpu.make_async_remote_copy(
            src_ref=grams.at[pair], dst_ref=parts.at[me], send_sem=gram_send.at[pair], recv_sem=gram_recv.at[me],
            device_id={"row": pair},
        )

    def gram_arrival(source):
        return pltpu.make_async_remote_copy(
            src_ref=parts.at[source], dst_ref=parts.at[source], send_sem=gram_send.at[0],
            recv_sem=gram_recv.at[source], device_id={"row": partner},
        )

    def turn_copy(other):
        target = jnp.where(other == chip, partner, 2 * other + core)
        return pltpu.make_async_remote_copy(
            src_ref=turns.at[me], dst_ref=turns.at[me], send_sem=turn_send.at[other], recv_sem=turn_recv.at[me],
            device_id={"row": target},
        )

    def pass_copy(pair):
        return pltpu.make_async_remote_copy(
            src_ref=turns.at[pair], dst_ref=turns.at[pair], send_sem=pass_send.at[pair], recv_sem=turn_recv.at[pair],
            device_id={"row": partner},
        )

    def edge_left(after):
        return pltpu.make_async_remote_copy(
            src_ref=edges.at[0], dst_ref=x.at[after, pl.ds(last * PAIR + BLOCK, BLOCK)], send_sem=edge_send.at[0],
            recv_sem=edge_recv.at[after, 0], device_id={"col": position - 1},
        )

    def edge_right(after):
        return pltpu.make_async_remote_copy(
            src_ref=edges.at[1], dst_ref=x.at[after, pl.ds(0, BLOCK)], send_sem=edge_send.at[1],
            recv_sem=edge_recv.at[after, 1], device_id={"col": position + 1},
        )

    def wait_edges(now):
        @pl.when(has_left)
        def _():
            edge_right(now).wait_recv()

        @pl.when(has_right)
        def _():
            edge_left(now).wait_recv()

    def take_gram(pair, now):
        base = pl.multiple_of(pair * PAIR, PAIR)
        block = x[now, pl.ds(base, PAIR), :]
        cross = lax.dot_general(
            block[:BLOCK], block[BLOCK:], (((1,), (1,)), ((), ())), precision=HIGHEST,
            preferred_element_type=jnp.float32,
        )
        squares = block * block
        partial = squares[:, :128]
        for lane in range(1, squares.shape[1] // 128):
            partial = partial + squares[:, lane * 128 : (lane + 1) * 128]
        norms = jnp.sum(partial.T, axis=0, keepdims=True)
        grams[pair, :HALF, :] = jnp.concatenate([cross[:HALF], cross[HALF:]], axis=1)
        grams[pair, HALF:, :] = jnp.broadcast_to(norms, (8, PAIR))

        @pl.when(pair != me)
        def _():
            gram_copy(pair).start()

    def own():
        def gather(source, carry):
            @pl.when(source != me)
            def _():
                gram_arrival(source).wait_recv()
            return carry

        lax.fori_loop(0, rows, gather, 0)
        total = grams[me]
        for source in range(rows):
            total = total + jnp.where(source == me, 0.0, parts[source])
        turns[me] = turn_transposed(total)

        def spread_out(other, carry):
            turn_copy(other).start()
            return carry

        lax.fori_loop(0, rows // 2, spread_out, 0)

    def take_turn(pair):
        @pl.when(pair != me)
        def _():
            pass_copy(pair).wait_recv()

            @pl.when(lax.rem(pair, 2) == core)
            def _():
                pass_copy(pair).start()

    def apply(pair, now):
        base = pl.multiple_of(pair * PAIR, PAIR)
        return mm4(unpacked(turns[pair]), x[now, pl.ds(base, PAIR), :])

    def step(index, carry):
        now = lax.rem(index, 2)
        after = 1 - now

        def inner_gram(pair, carry):
            take_gram(pair, now)
            return carry

        lax.fori_loop(1, last, inner_gram, 0)
        @pl.when(index > 0)
        def _():
            wait_edges(now)

        def edge_gram(which, carry):
            take_gram(which * last, now)
            return carry

        lax.fori_loop(0, 2, edge_gram, 0)

        @pl.when(me < pairs)
        def _():
            own()

        @pl.when(jnp.logical_and(index > 0, has_left))
        def _():
            edge_left(after).wait_send()

        take_turn(0)
        turned = apply(0, now)
        x[after, pl.ds(pl.multiple_of(jnp.where(has_left, PAIR, 0), BLOCK), BLOCK), :] = turned[:BLOCK]

        @pl.when(has_left)
        def _():
            edges[0] = turned[BLOCK:]
            edge_left(after).start()

        @pl.when(jnp.logical_not(has_left))
        def _():
            x[after, pl.ds(PAIR, BLOCK), :] = turned[BLOCK:]

        @pl.when(jnp.logical_and(index > 0, has_right))
        def _():
            edge_right(after).wait_send()

        take_turn(last)
        turned_last = apply(last, now)
        x[after, pl.ds((last - 1) * PAIR + BLOCK, BLOCK), :] = turned_last[BLOCK:]

        @pl.when(has_right)
        def _():
            edges[1] = turned_last[:BLOCK]
            edge_right(after).start()

        @pl.when(jnp.logical_not(has_right))
        def _():
            x[after, pl.ds(last * PAIR + BLOCK, BLOCK), :] = turned_last[:BLOCK]

        def inner_apply(pair, carry):
            take_turn(pair)
            turned = apply(pair, now)
            x[after, pl.ds(pl.multiple_of((pair + 1) * PAIR, PAIR), BLOCK), :] = turned[:BLOCK]
            x[after, pl.ds(pl.multiple_of((pair - 1) * PAIR + BLOCK, BLOCK), BLOCK), :] = turned[BLOCK:]
            return carry

        lax.fori_loop(1, last, inner_apply, 0)

        def settle(pair, carry):
            @pl.when(pair != me)
            def _():
                gram_copy(pair).wait_send()

                @pl.when(lax.rem(pair, 2) == core)
                def _():
                    pass_copy(pair).wait_send()
            return carry

        lax.fori_loop(0, pairs, settle, 0)

        @pl.when(me < pairs)
        def _():
            def settle_turn(other, carry):
                turn_copy(other).wait_send()
                return carry

            lax.fori_loop(0, rows // 2, settle_turn, 0)

        return carry

    lax.fori_loop(0, STEPS, step, 0)
    final = STEPS % 2

    def out_copy(start, size, which):
        return pltpu.make_async_copy(
            x.at[final, pl.ds(start, size)], out_ref.at[pl.ds(start, size)], out_sem.at[which]
        )

    middle = out_copy(BLOCK, width - PAIR, 0)
    middle.start()
    wait_edges(final)
    first = out_copy(0, BLOCK, 1)
    first.start()
    ending = out_copy(width - BLOCK, BLOCK, 2)
    ending.start()

    @pl.when(has_left)
    def _():
        edge_left(final).wait_send()

    @pl.when(has_right)
    def _():
        edge_right(final).wait_send()

    middle.wait()
    first.wait()
    ending.wait()


def solution(mesh):
    rows, cols = mesh.shape["row"], mesh.shape["col"]

    def local(columns, block_order):
        width, length = columns.shape
        pairs = width // PAIR
        assert 3 <= pairs <= rows and rows % 2 == 0
        dma = pltpu.SemaphoreType.DMA
        return pl.pallas_call(
            functools.partial(kernel, rows, cols, pairs),
            out_shape=jax.ShapeDtypeStruct((width, length), jnp.float32),
            in_specs=[pl.BlockSpec(memory_space=pltpu.SMEM), pl.BlockSpec(memory_space=pltpu.VMEM)],
            out_specs=pl.BlockSpec(memory_space=pl.ANY),
            scratch_shapes=[
                pltpu.VMEM((2, width, length), jnp.float32),
                pltpu.VMEM((pairs, PACKED, PAIR), jnp.float32),
                pltpu.VMEM((rows, PACKED, PAIR), jnp.float32),
                pltpu.VMEM((pairs, BLOCK + 8, PAIR), jnp.float32),
                pltpu.VMEM((2, BLOCK, length), jnp.float32),
                dma((pairs,)),
                dma((rows,)),
                dma((rows // 2,)),
                dma((pairs,)),
                dma((pairs,)),
                dma((2,)),
                dma((2, 2)),
                dma((3,)),
            ],
            compiler_params=pltpu.CompilerParams(
                collective_id=0, has_side_effects=True, vmem_limit_bytes=56 * 1024 * 1024
            ),
        )(block_order, columns.reshape(2 * pairs, BLOCK, length))

    placed = (P("col", "row"), P("col"))
    return jax.shard_map(local, mesh=mesh, in_specs=placed, out_specs=P("col", "row"), check_vma=False)
```

profile of v0, /device:TPU:0, one launch (start us, length us, event | category | flops | bytes accessed | tf_op | source)
XLA Modules:
  0.0 99.7 jit_solution(13647535191169778777)
XLA Ops:
  0.0 94.9 %shard_map.28 = f32[1024,1024]{1,0:T(8,128)} custom-call(s32[16]{0:T(128)} %order_ref.1, f32[16,64,1024]{2,1,0:T(8,128)} %bitcast.1), custom_call_target="tpu_custom_call" | custom-call | tf_op jit(solution)/shard_map/pallas_call | solution.py:373
  94.9 4.8 %copy.4 = f32[1024,1024]{1,0:T(8,128)} copy(f32[1024,1024]{1,0:T(8,128)} %shard_map.28) | data formatting | bytes 8388608
where the time goes:
time: 101 us; the launch traced here: 99.7 us
  Pallas kernels  94.9 us (94%)
  local copies, waits for them, and re-layouts  4.79 us (5%)
    pallas_call x1, Pallas kernels, local(): pl.pallas_call(functools.partial(kernel, rows, cols, pairs), out_shape=ja...  94.9 us
    unnamed x1, local copies, waits for them, and re-layouts  4.79 us

commit v1 on v0

v1 whole, which is shorter than its diff:
```python
import functools

import jax
import jax.numpy as jnp
from jax import lax
from jax.experimental import pallas as pl
from jax.experimental.pallas import tpu as pltpu
from jax.sharding import PartitionSpec as P

BLOCK = 64
PAIR = 2 * BLOCK
STEPS = 4
HALF = BLOCK // 2
PACKED = HALF + 8
UPPER = 1.0 + BLOCK * BLOCK * 0.0905
NN = (((1,), (0,)), ((), ()))
NT = (((1,), (1,)), ((), ()))


def split(a):
    high = a.astype(jnp.bfloat16)
    return high, (a - high.astype(jnp.float32)).astype(jnp.bfloat16)


def split3(a):
    high = a.astype(jnp.bfloat16)
    rest = a - high.astype(jnp.float32)
    middle = rest.astype(jnp.bfloat16)
    return high, middle, (rest - middle.astype(jnp.float32)).astype(jnp.bfloat16)


def product(a, b, dims=NN):
    return lax.dot_general(a, b, dims, preferred_element_type=jnp.float32)


def mm3(a, b):
    (ah, am), (bh, bm) = split(a), split(b)
    count = a.shape[0]
    stacked = product(jnp.concatenate([ah, am], axis=0), bh)
    return stacked[:count] + stacked[count:] + product(ah, bm)


def mm6(a, b, dims=NN):
    (ah, am, al), (bh, bm, bl) = split3(a), split3(b)
    count = a.shape[0]
    first = product(jnp.concatenate([ah, am, al], axis=0), bh, dims)
    second = product(jnp.concatenate([ah, am], axis=0), bm, dims)
    small = first[2 * count :] + second[count:] + product(ah, bl, dims)
    return first[:count] + ((first[count : 2 * count] + second[:count]) + small)


def left(a):
    return a[:, :BLOCK]


def inverse(system, eye):
    low = 2.0 / (1.0 + UPPER)
    y = system * low
    reach = low * (2.0 - low)
    scale = 2.0 / (1.0 + reach)
    x = (scale * low) * (2.0 * eye - y)
    y = scale * (2.0 * y - mm3(left(y), y))
    low = scale * reach
    while low < 0.999:
        reach = low * (2.0 - low)
        scale = 2.0 / (1.0 + reach)
        following = scale * (2.0 * y - mm3(left(y), y))
        x = scale * (2.0 * x - mm3(left(x), y))
        y = following
        low = scale * reach
    return x


def turn_packed(total):
    row = lax.broadcasted_iota(jnp.int32, (HALF, PAIR), 0)
    lane = lax.broadcasted_iota(jnp.int32, (HALF, PAIR), 1)
    cross = total[:HALF]
    norms = total[HALF : HALF + 1]
    bottom_norms = total[HALF + 1 : HALF + 2]
    upper_norms = jnp.sum(jnp.where(lane == row, norms, 0.0), axis=1, keepdims=True)
    lower_norms = jnp.sum(jnp.where(lane == row + HALF, norms, 0.0), axis=1, keepdims=True)
    top_norms = jnp.where(lane < BLOCK, upper_norms, lower_norms)
    spread = bottom_norms - top_norms
    square = spread * spread + 4.0 * cross * cross
    radius = jnp.sqrt(square)
    scale_term = (top_norms + bottom_norms) / BLOCK
    packed = 2.0 * cross * spread / (square + jnp.abs(spread) * radius + scale_term * scale_term)
    rolled = pltpu.roll(packed, BLOCK, 1)
    coupling = jnp.concatenate([jnp.where(lane < BLOCK, packed, rolled), jnp.where(lane < BLOCK, rolled, packed)], axis=0)
    rows = lax.broadcasted_iota(jnp.int32, (BLOCK, PAIR), 0)
    lanes = lax.broadcasted_iota(jnp.int32, (BLOCK, PAIR), 1)
    columns = jnp.where(lanes < BLOCK, lanes, lanes - BLOCK)
    eye = jnp.where(rows == columns, 1.0, 0.0).astype(jnp.float32)
    narrow = left(coupling)
    narrow_t = narrow.T
    system = eye + mm6(narrow, jnp.concatenate([narrow, narrow], axis=0), NT)
    x = inverse(system, eye)
    lower = mm6(narrow_t, x)
    residual = eye - x - mm6(narrow, lower)
    stacked = jnp.concatenate([x, lower], axis=0)
    stacked = stacked + mm3(left(stacked), residual)
    x, lower = stacked[:BLOCK], 2.0 * stacked[BLOCK:]
    corner = eye - mm6(left(lower), coupling)
    diagonal = jnp.sum(jnp.where(rows == columns, corner, 0.0), axis=0, keepdims=True)
    mixed = jnp.where(rows <= columns, 2.0 * x - eye, corner)
    body = jnp.where(lanes < BLOCK, mixed, lower)
    return jnp.concatenate([body, jnp.broadcast_to(diagonal, (8, PAIR))], axis=0)


def unpacked(packed):
    rows = lax.broadcasted_iota(jnp.int32, (BLOCK, PAIR), 0)
    lanes = lax.broadcasted_iota(jnp.int32, (BLOCK, PAIR), 1)
    columns = jnp.where(lanes < BLOCK, lanes, lanes - BLOCK)
    body = packed[:BLOCK]
    flipped = jnp.concatenate([body, body], axis=0).T
    mixed_t, lower_t = flipped[:BLOCK], flipped[BLOCK:]
    moved = pltpu.roll(body, BLOCK, 1)
    top = jnp.where(lanes < BLOCK, jnp.where(rows > columns, mixed_t, body), -lower_t)
    corner = jnp.where(rows == columns, packed[BLOCK : BLOCK + 1], jnp.where(rows > columns, moved, mixed_t))
    bottom = jnp.where(lanes < BLOCK, moved, corner)
    return jnp.concatenate([top, bottom], axis=0)


def gram_packed(block):
    high, low = split(block)
    lefts = jnp.concatenate([high[:BLOCK], low[:BLOCK]], axis=0)
    rights = jnp.concatenate([high[BLOCK:], low[BLOCK:]], axis=0)
    parts = product(lefts, rights, NT)
    halves = parts[:BLOCK] + parts[BLOCK:]
    cross = halves + pltpu.roll(halves, BLOCK, 1)
    lane = lax.broadcasted_iota(jnp.int32, (HALF, PAIR), 1)
    cross = jnp.where(lane < BLOCK, cross[:HALF], cross[HALF:])
    squares = block * block
    partial = squares[:, :128]
    for start in range(128, squares.shape[1], 128):
        partial = partial + squares[:, start : start + 128]
    norms = jnp.broadcast_to(jnp.sum(partial.T, axis=0, keepdims=True), (8, PAIR))
    rows = lax.broadcasted_iota(jnp.int32, (8, PAIR), 0)
    lanes = lax.broadcasted_iota(jnp.int32, (8, PAIR), 1)
    norms = jnp.where(jnp.logical_and(rows == 1, lanes < BLOCK), pltpu.roll(norms, BLOCK, 1), norms)
    return jnp.concatenate([cross, norms], axis=0)


def turned(packed, block):
    high, low = split(block)
    turn_high, turn_middle, turn_low = split3(unpacked(packed))
    lefts = jnp.concatenate([turn_high, turn_middle, turn_low, turn_high], axis=1)
    return product(lefts, jnp.concatenate([high, high, high, low], axis=0))


def kernel(rows, cols, pairs, order_ref, columns_ref, out_ref, raw, x0, x1, grams, parts, turns, edges,
           gram_send, gram_recv, turn_send, turn_recv, pass_send, edge_send, edge_recv, in_sem, out_sem):
    buffers = (x0, x1)
    arrival = pltpu.make_async_copy(columns_ref, raw, in_sem)
    arrival.start()
    me = lax.axis_index("row")
    position = lax.axis_index("col")
    core = lax.rem(me, 2)
    chip = lax.div(me, 2)
    partner = me + 1 - 2 * core
    has_left = position > 0
    has_right = position < cols - 1
    last = pairs - 1
    width = pairs * PAIR

    barrier = pltpu.get_barrier_semaphore()

    def greet(other, carry):
        @pl.when(other != me)
        def _():
            pl.semaphore_signal(barrier, inc=1, device_id={"row": other})
        return carry

    lax.fori_loop(0, rows, greet, 0)

    @pl.when(has_left)
    def _():
        pl.semaphore_signal(barrier, inc=1, device_id={"col": position - 1})

    @pl.when(has_right)
    def _():
        pl.semaphore_signal(barrier, inc=1, device_id={"col": position + 1})

    def fill(slot, carry):
        source = lax.rem(order_ref[slot], 2 * pairs)
        x0[pl.ds(pl.multiple_of(slot * BLOCK, BLOCK), BLOCK), :] = raw[source]
        return carry

    arrival.wait()
    lax.fori_loop(0, 2 * pairs, fill, 0)

    greeted = rows - 1 + has_left.astype(jnp.int32) + has_right.astype(jnp.int32)
    pl.semaphore_wait(barrier, greeted)

    def gram_copy(pair):
        return pltpu.make_async_remote_copy(
            src_ref=grams.at[pair], dst_ref=parts.at[me], send_sem=gram_send.at[pair], recv_sem=gram_recv.at[me],
            device_id={"row": pair},
        )

    def gram_arrival(source):
        return pltpu.make_async_remote_copy(
            src_ref=parts.at[source], dst_ref=parts.at[source], send_sem=gram_send.at[0],
            recv_sem=gram_recv.at[source], device_id={"row": partner},
        )

    def turn_copy(other):
        target = jnp.where(other == chip, partner, 2 * other + core)
        return pltpu.make_async_remote_copy(
            src_ref=turns.at[me], dst_ref=turns.at[me], send_sem=turn_send.at[other], recv_sem=turn_recv.at[me],
            device_id={"row": target},
        )

    def pass_copy(pair):
        return pltpu.make_async_remote_copy(
            src_ref=turns.at[pair], dst_ref=turns.at[pair], send_sem=pass_send.at[pair], recv_sem=turn_recv.at[pair],
            device_id={"row": partner},
        )

    def edge_left(after):
        return pltpu.make_async_remote_copy(
            src_ref=edges.at[0], dst_ref=buffers[after].at[pl.ds(last * PAIR + BLOCK, BLOCK)], send_sem=edge_send.at[0],
            recv_sem=edge_recv.at[after, 0], device_id={"col": position - 1},
        )

    def edge_right(after):
        return pltpu.make_async_remote_copy(
            src_ref=edges.at[1], dst_ref=buffers[after].at[pl.ds(0, BLOCK)], send_sem=edge_send.at[1],
            recv_sem=edge_recv.at[after, 1], device_id={"col": position + 1},
        )

    def wait_edges(now):
        @pl.when(has_left)
        def _():
            edge_right(now).wait_recv()

        @pl.when(has_right)
        def _():
            edge_left(now).wait_recv()

    def block_of(pair, now):
        return buffers[now][pl.ds(pl.multiple_of(pair * PAIR, PAIR), PAIR), :]

    def take_grams(first, second, now):
        for pair in (first, second):
            grams[pair] = gram_packed(block_of(pair, now))
        for pair in (first, second):
            @pl.when(pair != me)
            def _(pair=pair):
                gram_copy(pair).start()

    def own():
        def gather(source, carry):
            @pl.when(source != me)
            def _():
                gram_arrival(source).wait_recv()
            return carry

        lax.fori_loop(0, rows, gather, 0)
        total = grams[me]
        for source in range(rows):
            total = total + jnp.where(source == me, 0.0, parts[source])
        turns[me] = turn_packed(total)

        def spread_out(other, carry):
            turn_copy(other).start()
            return carry

        lax.fori_loop(0, rows // 2, spread_out, 0)

    def take_turn(pair):
        @pl.when(pair != me)
        def _():
            pass_copy(pair).wait_recv()

            @pl.when(lax.rem(pair, 2) == core)
            def _():
                pass_copy(pair).start()

    def step(index, now):
        after = 1 - now
        later = buffers[after]

        def inner_gram(group, carry):
            take_grams(2 * group + 1, 2 * group + 2, now)
            return carry

        lax.fori_loop(0, (pairs - 2) // 2, inner_gram, 0)

        @pl.when(index > 0)
        def _():
            wait_edges(now)

        take_grams(0, last, now)

        @pl.when(me < pairs)
        def _():
            own()

        @pl.when(jnp.logical_and(index > 0, has_left))
        def _():
            edge_left(after).wait_send()

        @pl.when(jnp.logical_and(index > 0, has_right))
        def _():
            edge_right(after).wait_send()

        take_turn(0)
        take_turn(last)
        first_turned = turned(turns[0], block_of(0, now))
        last_turned = turned(turns[last], block_of(last, now))
        later[pl.ds(pl.multiple_of(jnp.where(has_left, PAIR, 0), BLOCK), BLOCK), :] = first_turned[:BLOCK]
        edges[0] = first_turned[BLOCK:]
        edges[1] = last_turned[:BLOCK]
        later[pl.ds((last - 1) * PAIR + BLOCK, BLOCK), :] = last_turned[BLOCK:]

        @pl.when(has_left)
        def _():
            edge_left(after).start()

        @pl.when(jnp.logical_not(has_left))
        def _():
            later[pl.ds(PAIR, BLOCK), :] = edges[0]

        @pl.when(has_right)
        def _():
            edge_right(after).start()

        @pl.when(jnp.logical_not(has_right))
        def _():
            later[pl.ds(last * PAIR + BLOCK, BLOCK), :] = edges[1]

        def inner_apply(group, carry):
            chosen = (2 * group + 1, 2 * group + 2)
            for pair in chosen:
                take_turn(pair)
            for pair in chosen:
                result = turned(turns[pair], block_of(pair, now))
                later[pl.ds(pl.multiple_of((pair + 1) * PAIR, PAIR), BLOCK), :] = result[:BLOCK]
                later[pl.ds(pl.multiple_of((pair - 1) * PAIR + BLOCK, BLOCK), BLOCK), :] = result[BLOCK:]
            return carry

        lax.fori_loop(0, (pairs - 2) // 2, inner_apply, 0)

        def settle(pair, carry):
            @pl.when(pair != me)
            def _():
                gram_copy(pair).wait_send()

                @pl.when(lax.rem(pair, 2) == core)
                def _():
                    pass_copy(pair).wait_send()
            return carry

        lax.fori_loop(0, pairs, settle, 0)

        @pl.when(me < pairs)
        def _():
            def settle_turn(other, carry):
                turn_copy(other).wait_send()
                return carry

            lax.fori_loop(0, rows // 2, settle_turn, 0)

    def two_steps(index, carry):
        step(2 * index, 0)
        step(2 * index + 1, 1)
        return carry

    lax.fori_loop(0, STEPS // 2, two_steps, 0)
    final = STEPS % 2

    def out_copy(start, size, which):
        return pltpu.make_async_copy(
            buffers[final].at[pl.ds(start, size)], out_ref.at[pl.ds(start, size)], out_sem.at[which]
        )

    middle = out_copy(BLOCK, width - PAIR, 0)
    middle.start()
    wait_edges(final)
    first = out_copy(0, BLOCK, 1)
    first.start()
    ending = out_copy(width - BLOCK, BLOCK, 2)
    ending.start()

    @pl.when(has_left)
    def _():
        edge_left(final).wait_send()

    @pl.when(has_right)
    def _():
        edge_right(final).wait_send()

    middle.wait()
    first.wait()
    ending.wait()


def solution(mesh):
    rows, cols = mesh.shape["row"], mesh.shape["col"]

    def local(columns, block_order):
        width, length = columns.shape
        pairs = width // PAIR
        assert 4 <= pairs <= rows and rows % 2 == 0 and pairs % 2 == 0
        dma = pltpu.SemaphoreType.DMA
        return pl.pallas_call(
            functools.partial(kernel, rows, cols, pairs),
            out_shape=jax.ShapeDtypeStruct((width, length), jnp.float32),
            in_specs=[pl.BlockSpec(memory_space=pltpu.SMEM), pl.BlockSpec(memory_space=pl.ANY)],
            out_specs=pl.BlockSpec(memory_space=pl.ANY),
            scratch_shapes=[
                pltpu.VMEM((2 * pairs, BLOCK, length), jnp.float32),
                pltpu.VMEM((width, length), jnp.float32),
                pltpu.VMEM((width, length), jnp.float32),
                pltpu.VMEM((pairs, PACKED, PAIR), jnp.float32),
                pltpu.VMEM((rows, PACKED, PAIR), jnp.float32),
                pltpu.VMEM((pairs, BLOCK + 8, PAIR), jnp.float32),
                pltpu.VMEM((2, BLOCK, length), jnp.float32),
                dma((pairs,)),
                dma((rows,)),
                dma((rows // 2,)),
                dma((pairs,)),
                dma((pairs,)),
                dma((2,)),
                dma((2, 2)),
                dma,
                dma((3,)),
            ],
            compiler_params=pltpu.CompilerParams(
                collective_id=0, has_side_effects=True, vmem_limit_bytes=56 * 1024 * 1024
            ),
        )(block_order, columns.reshape(2 * pairs, BLOCK, length))

    placed = (P("col", "row"), P("col"))
    return jax.shard_map(local, mesh=mesh, in_specs=placed, out_specs=P("col", "row"), check_vma=False)
```

time: 101 us -> 86.5 us (0.86)
  Pallas kernels: 94.9 us -> 80.9 us
    pallas_call x1, Pallas kernels: 94.9 us -> 80.9 us  [local(): pl.pallas_call(functools.partial(kernel, rows, cols, pairs), out_shape=ja...]
where the time goes in v1:
time: 86.5 us; the launch traced here: 85.7 us
  Pallas kernels  80.9 us (94%)
  local copies, waits for them, and re-layouts  4.79 us (6%)
    pallas_call x1, Pallas kernels, local(): pl.pallas_call(functools.partial(kernel, rows, cols, pairs), out_shape=ja...  80.9 us
    unnamed x1, local copies, waits for them, and re-layouts  4.79 us

profile of v1, /device:TPU:0, one launch (start us, length us, event | category | flops | bytes accessed | tf_op | source)
XLA Modules:
  0.0 85.7 jit_solution(18131979882088262040)
XLA Ops:
  0.0 80.9 %shard_map.28 = f32[1024,1024]{1,0:T(8,128)} custom-call(s32[16]{0:T(128)} %order_ref.1, f32[16,64,1024]{2,1,0:T(8,128)} %bitcast.1), custom_call_target="tpu_custom_call" | custom-call | tf_op jit(solution)/shard_map/pallas_call | solution.py:407
  80.9 4.8 %copy.4 = f32[1024,1024]{1,0:T(8,128)} copy(f32[1024,1024]{1,0:T(8,128)} %shard_map.28) | data formatting | bytes 8388608

commit v2 on v1

--- a/solution.py
+++ b/solution.py
@@ -141,15 +141,25 @@
     return jnp.concatenate([cross, norms], axis=0)
 
 
-def turned(packed, block):
+def apply_turn(matrix, block):
     high, low = split(block)
-    turn_high, turn_middle, turn_low = split3(unpacked(packed))
+    turn_high, turn_middle, turn_low = split3(matrix)
     lefts = jnp.concatenate([turn_high, turn_middle, turn_low, turn_high], axis=1)
     return product(lefts, jnp.concatenate([high, high, high, low], axis=0))
 
 
-def kernel(rows, cols, pairs, order_ref, columns_ref, out_ref, raw, x0, x1, grams, parts, turns, edges,
-           gram_send, gram_recv, turn_send, turn_recv, pass_send, edge_send, edge_recv, in_sem, out_sem):
+def turned(packed, block):
+    return apply_turn(unpacked(packed), block)
+
+
+def turned_half(packed, block, side):
+    matrix = unpacked(packed)
+    return apply_turn(matrix[:BLOCK] if side == 0 else matrix[BLOCK:], block)
+
+
+def kernel(rows, cols, pairs, order_ref, columns_ref, out_ref, raw, x0, x1, grams, parts, turns, halos,
+           gram_send, gram_recv, turn_send, turn_recv, pass_send, halo_send, halo_recv, relay_send,
+           start_send, start_recv, edge_send, edge_recv, in_sem, out_sem):
     buffers = (x0, x1)
     arrival = pltpu.make_async_copy(columns_ref, raw, in_sem)
     arrival.start()
@@ -158,10 +168,14 @@
     core = lax.rem(me, 2)
     chip = lax.div(me, 2)
     partner = me + 1 - 2 * core
+    base = lax.rem(me, pairs)
     has_left = position > 0
     has_right = position < cols - 1
+    has = (has_left, has_right)
+    beside = (position - 1, position + 1)
     last = pairs - 1
-    width = pairs * PAIR
+    direct = (last % 2, 0)
+    half = rows // 2
 
     barrier = pltpu.get_barrier_semaphore()
 
@@ -169,27 +183,23 @@
         @pl.when(other != me)
         def _():
             pl.semaphore_signal(barrier, inc=1, device_id={"row": other})
+
+        for side in (0, 1):
+            @pl.when(has[side])
+            def _(side=side):
+                pl.semaphore_signal(barrier, inc=1, device_id={"row": other, "col": beside[side]})
         return carry
 
     lax.fori_loop(0, rows, greet, 0)
-
-    @pl.when(has_left)
-    def _():
-        pl.semaphore_signal(barrier, inc=1, device_id={"col": position - 1})
-
-    @pl.when(has_right)
-    def _():
-        pl.semaphore_signal(barrier, inc=1, device_id={"col": position + 1})
 
     def fill(slot, carry):
         source = lax.rem(order_ref[slot], 2 * pairs)
-        x0[pl.ds(pl.multiple_of(slot * BLOCK, BLOCK), BLOCK), :] = raw[source]
+        x0[pl.ds(pl.multiple_of(slot * BLOCK + PAIR, BLOCK), BLOCK), :] = raw[source]
         return carry
 
     arrival.wait()
     lax.fori_loop(0, 2 * pairs, fill, 0)
-
-    greeted = rows - 1 + has_left.astype(jnp.int32) + has_right.astype(jnp.int32)
+    greeted = rows - 1 + rows * (has_left.astype(jnp.int32) + has_right.astype(jnp.int32))
     pl.semaphore_wait(barrier, greeted)
 
     def gram_copy(pair):
@@ -217,37 +227,44 @@
             device_id={"row": partner},
         )
 
-    def edge_left(after):
-        return pltpu.make_async_remote_copy(
-            src_ref=edges.at[0], dst_ref=buffers[after].at[pl.ds(last * PAIR + BLOCK, BLOCK)], send_sem=edge_send.at[0],
-            recv_sem=edge_recv.at[after, 0], device_id={"col": position - 1},
-        )
-
-    def edge_right(after):
-        return pltpu.make_async_remote_copy(
-            src_ref=edges.at[1], dst_ref=buffers[after].at[pl.ds(0, BLOCK)], send_sem=edge_send.at[1],
-            recv_sem=edge_recv.at[after, 1], device_id={"col": position + 1},
-        )
-
-    def wait_edges(now):
-        @pl.when(has_left)
-        def _():
-            edge_right(now).wait_recv()
-
-        @pl.when(has_right)
-        def _():
-            edge_left(now).wait_recv()
-
-    def block_of(pair, now):
-        return buffers[now][pl.ds(pl.multiple_of(pair * PAIR, PAIR), PAIR), :]
-
-    def take_grams(first, second, now):
-        for pair in (first, second):
-            grams[pair] = gram_packed(block_of(pair, now))
-        for pair in (first, second):
-            @pl.when(pair != me)
-            def _(pair=pair):
-                gram_copy(pair).start()
+    def halo_copy(other, side, now):
+        return pltpu.make_async_remote_copy(
+            src_ref=turns.at[me], dst_ref=halos.at[now, side], send_sem=halo_send.at[other],
+            recv_sem=halo_recv.at[now, side], device_id={"row": 2 * other + core, "col": beside[1 - side]},
+        )
+
+    def relay_copy(side, now):
+        return pltpu.make_async_remote_copy(
+            src_ref=halos.at[now, side], dst_ref=halos.at[now, side], send_sem=relay_send.at[side],
+            recv_sem=halo_recv.at[now, side], device_id={"row": partner},
+        )
+
+    far = (pairs + 1) * PAIR
+
+    def start_copy(side):
+        source = pairs * PAIR if side == 0 else PAIR
+        target = 0 if side == 0 else far
+        return pltpu.make_async_remote_copy(
+            src_ref=x0.at[pl.ds(source, PAIR)], dst_ref=x0.at[pl.ds(target, PAIR)], send_sem=start_send.at[side],
+            recv_sem=start_recv.at[side], device_id={"col": beside[1 - side]},
+        )
+
+    def edge_copy(side, after):
+        source = pairs * PAIR if side == 0 else PAIR + BLOCK
+        target = 0 if side == 0 else far + BLOCK
+        return pltpu.make_async_remote_copy(
+            src_ref=buffers[after].at[pl.ds(source, BLOCK)], dst_ref=buffers[after].at[pl.ds(target, BLOCK)],
+            send_sem=edge_send.at[after, side], recv_sem=edge_recv.at[after, side],
+            device_id={"col": beside[1 - side]},
+        )
+
+    for side in (0, 1):
+        @pl.when(has[1 - side])
+        def _(side=side):
+            start_copy(side).start()
+
+    def slot_of(slot, now):
+        return buffers[now][pl.ds(pl.multiple_of(slot * PAIR, PAIR), PAIR), :]
 
     def own():
         def gather(source, carry):
@@ -262,85 +279,141 @@
             total = total + jnp.where(source == me, 0.0, parts[source])
         turns[me] = turn_packed(total)
 
-        def spread_out(other, carry):
-            turn_copy(other).start()
-            return carry
-
-        lax.fori_loop(0, rows // 2, spread_out, 0)
-
-    def take_turn(pair):
-        @pl.when(pair != me)
-        def _():
-            pass_copy(pair).wait_recv()
-
-            @pl.when(lax.rem(pair, 2) == core)
-            def _():
-                pass_copy(pair).start()
-
     def step(index, now):
         after = 1 - now
         later = buffers[after]
 
-        def inner_gram(group, carry):
-            take_grams(2 * group + 1, 2 * group + 2, now)
+        def take_grams(group, carry):
+            chosen = (2 * group, 2 * group + 1)
+            for pair in chosen:
+                grams[pair] = gram_packed(slot_of(pair + 1, now))
+            for pair in chosen:
+                @pl.when(pair != me)
+                def _(pair=pair):
+                    gram_copy(pair).start()
             return carry
 
-        lax.fori_loop(0, (pairs - 2) // 2, inner_gram, 0)
-
-        @pl.when(index > 0)
-        def _():
-            wait_edges(now)
-
-        take_grams(0, last, now)
+        lax.fori_loop(0, pairs // 2, take_grams, 0)
 
         @pl.when(me < pairs)
         def _():
             own()
 
-        @pl.when(jnp.logical_and(index > 0, has_left))
+            def spread_out(other, carry):
+                turn_copy(other).start()
+                return carry
+
+            lax.fori_loop(0, half, spread_out, 0)
+
+        for side, owner in ((0, last), (1, 0)):
+            @pl.when(jnp.logical_and(me == owner, has[1 - side]))
+            def _(side=side):
+                def spread_halo(other, carry):
+                    halo_copy(other, side, now).start()
+                    return carry
+
+                lax.fori_loop(0, half, spread_halo, 0)
+
+        @pl.when(index > 1)
         def _():
-            edge_left(after).wait_send()
-
-        @pl.when(jnp.logical_and(index > 0, has_right))
+            for side in (0, 1):
+                @pl.when(has[1 - side])
+                def _(side=side):
+                    edge_copy(side, after).wait_send()
+
+        if now == 1:
+            @pl.when(index == 1)
+            def _():
+                for side in (0, 1):
+                    @pl.when(has[1 - side])
+                    def _(side=side):
+                        start_copy(side).wait_send()
+
+        def receive(pair):
+            @pl.when(pair != me)
+            def _():
+                pass_copy(pair).wait_recv()
+
+                @pl.when(lax.rem(pair, 2) == core)
+                def _():
+                    pass_copy(pair).start()
+
+        def receive_halo(side):
+            @pl.when(has[side])
+            def _():
+                relay_copy(side, now).wait_recv()
+
+                @pl.when(core == direct[side])
+                def _():
+                    relay_copy(side, now).start()
+
+        def pair_at(place):
+            even = 2 * (place - 1)
+            odd = 2 * (place - pairs // 2) + 1
+            shift = jnp.where(place < 2, place, jnp.where(place <= pairs // 2, even, odd))
+            return jnp.bitwise_xor(base, shift)
+
+        def apply_two(first, second):
+            results = [turned(turns[pair], slot_of(pair + 1, now)) for pair in (first, second)]
+            for pair, result in zip((first, second), results):
+                opening = jnp.logical_and(pair == 0, jnp.logical_not(has_left))
+                closing = jnp.logical_and(pair == last, jnp.logical_not(has_right))
+                top = jnp.where(opening, PAIR, jnp.where(closing, pairs * PAIR + BLOCK, (pair + 2) * PAIR))
+                bottom = jnp.where(opening, 2 * PAIR, pair * PAIR + BLOCK)
+                later[pl.ds(pl.multiple_of(top, BLOCK), BLOCK), :] = result[:BLOCK]
+                later[pl.ds(pl.multiple_of(bottom, BLOCK), BLOCK), :] = result[BLOCK:]
+
+        receive(pair_at(0))
+        receive(pair_at(1))
+        apply_two(pair_at(0), pair_at(1))
+
+        def receive_direct(place, carry):
+            receive(pair_at(place))
+            return carry
+
+        lax.fori_loop(2, pairs // 2 + 1, receive_direct, 0)
+        for side in (0, 1):
+            @pl.when(core == direct[side])
+            def _(side=side):
+                receive_halo(side)
+
+        def apply_rest(group, carry):
+            for place in (2 * group, 2 * group + 1):
+                @pl.when(place > pairs // 2)
+                def _(place=place):
+                    receive(pair_at(place))
+            apply_two(pair_at(2 * group), pair_at(2 * group + 1))
+            return carry
+
+        lax.fori_loop(1, pairs // 2, apply_rest, 0)
+        for side in (0, 1):
+            @pl.when(core != direct[side])
+            def _(side=side):
+                receive_halo(side)
+
+        for side in (0, 1):
+            @pl.when(has[side])
+            def _(side=side):
+                if now == 0:
+                    @pl.when(index == 0)
+                    def _():
+                        start_copy(side).wait_recv()
+
+                    @pl.when(index > 0)
+                    def _():
+                        edge_copy(side, now).wait_recv()
+                else:
+                    edge_copy(side, now).wait_recv()
+                rest = turned_half(halos[now, side], slot_of(side * (pairs + 1), now), side)
+                target = PAIR if side == 0 else pairs * PAIR + BLOCK
+                later[pl.ds(target, BLOCK), :] = rest
+
+        @pl.when(index < STEPS - 1)
         def _():
-            edge_right(after).wait_send()
-
-        take_turn(0)
-        take_turn(last)
-        first_turned = turned(turns[0], block_of(0, now))
-        last_turned = turned(turns[last], block_of(last, now))
-        later[pl.ds(pl.multiple_of(jnp.where(has_left, PAIR, 0), BLOCK), BLOCK), :] = first_turned[:BLOCK]
-        edges[0] = first_turned[BLOCK:]
-        edges[1] = last_turned[:BLOCK]
-        later[pl.ds((last - 1) * PAIR + BLOCK, BLOCK), :] = last_turned[BLOCK:]
-
-        @pl.when(has_left)
-        def _():
-            edge_left(after).start()
-
-        @pl.when(jnp.logical_not(has_left))
-        def _():
-            later[pl.ds(PAIR, BLOCK), :] = edges[0]
-
-        @pl.when(has_right)
-        def _():
-            edge_right(after).start()
-
-        @pl.when(jnp.logical_not(has_right))
-        def _():
-            later[pl.ds(last * PAIR + BLOCK, BLOCK), :] = edges[1]
-
-        def inner_apply(group, carry):
-            chosen = (2 * group + 1, 2 * group + 2)
-            for pair in chosen:
-                take_turn(pair)
-            for pair in chosen:
-                result = turned(turns[pair], block_of(pair, now))
-                later[pl.ds(pl.multiple_of((pair + 1) * PAIR, PAIR), BLOCK), :] = result[:BLOCK]
-                later[pl.ds(pl.multiple_of((pair - 1) * PAIR + BLOCK, BLOCK), BLOCK), :] = result[BLOCK:]
-            return carry
-
-        lax.fori_loop(0, (pairs - 2) // 2, inner_apply, 0)
+            for side in (0, 1):
+                @pl.when(has[1 - side])
+                def _(side=side):
+                    edge_copy(side, after).start()
 
         def settle(pair, carry):
             @pl.when(pair != me)
@@ -360,7 +433,20 @@
                 turn_copy(other).wait_send()
                 return carry
 
-            lax.fori_loop(0, rows // 2, settle_turn, 0)
+            lax.fori_loop(0, half, settle_turn, 0)
+
+        for side, owner in ((0, last), (1, 0)):
+            @pl.when(jnp.logical_and(me == owner, has[1 - side]))
+            def _(side=side):
+                def settle_halo(other, carry):
+                    halo_copy(other, side, now).wait_send()
+                    return carry
+
+                lax.fori_loop(0, half, settle_halo, 0)
+
+            @pl.when(jnp.logical_and(core == direct[side], has[side]))
+            def _(side=side):
+                relay_copy(side, now).wait_send()
 
     def two_steps(index, carry):
         step(2 * index, 0)
@@ -369,31 +455,14 @@
 
     lax.fori_loop(0, STEPS // 2, two_steps, 0)
     final = STEPS % 2
-
-    def out_copy(start, size, which):
-        return pltpu.make_async_copy(
-            buffers[final].at[pl.ds(start, size)], out_ref.at[pl.ds(start, size)], out_sem.at[which]
-        )
-
-    middle = out_copy(BLOCK, width - PAIR, 0)
-    middle.start()
-    wait_edges(final)
-    first = out_copy(0, BLOCK, 1)
-    first.start()
-    ending = out_copy(width - BLOCK, BLOCK, 2)
-    ending.start()
-
-    @pl.when(has_left)
-    def _():
-        edge_left(final).wait_send()
-
-    @pl.when(has_right)
-    def _():
-        edge_right(final).wait_send()
-
-    middle.wait()
-    first.wait()
-    ending.wait()
+    result = pltpu.make_async_copy(buffers[final].at[pl.ds(PAIR, pairs * PAIR)], out_ref, out_sem)
+    result.start()
+    for side in (0, 1):
+        @pl.when(has[1 - side])
+        def _(side=side):
+            edge_copy(side, 1 - final).wait_send()
+
+    result.wait()
 
 
 def solution(mesh):
@@ -402,8 +471,9 @@
     def local(columns, block_order):
         width, length = columns.shape
         pairs = width // PAIR
-        assert 4 <= pairs <= rows and rows % 2 == 0 and pairs % 2 == 0
+        assert 4 <= pairs <= rows and rows % pairs == 0 and pairs & (pairs - 1) == 0 and STEPS % 2 == 0
         dma = pltpu.SemaphoreType.DMA
+        buffer = pltpu.VMEM((width + 2 * PAIR, length), jnp.float32)
         return pl.pallas_call(
             functools.partial(kernel, rows, cols, pairs),
             out_shape=jax.ShapeDtypeStruct((width, length), jnp.float32),
@@ -411,21 +481,26 @@
             out_specs=pl.BlockSpec(memory_space=pl.ANY),
             scratch_shapes=[
                 pltpu.VMEM((2 * pairs, BLOCK, length), jnp.float32),
-                pltpu.VMEM((width, length), jnp.float32),
-                pltpu.VMEM((width, length), jnp.float32),
+                buffer,
+                buffer,
                 pltpu.VMEM((pairs, PACKED, PAIR), jnp.float32),
                 pltpu.VMEM((rows, PACKED, PAIR), jnp.float32),
                 pltpu.VMEM((pairs, BLOCK + 8, PAIR), jnp.float32),
-                pltpu.VMEM((2, BLOCK, length), jnp.float32),
+                pltpu.VMEM((2, 2, BLOCK + 8, PAIR), jnp.float32),
                 dma((pairs,)),
                 dma((rows,)),
                 dma((rows // 2,)),
                 dma((pairs,)),
                 dma((pairs,)),
+                dma((rows // 2,)),
+                dma((2, 2)),
+                dma((2,)),
+                dma((2,)),
                 dma((2,)),
                 dma((2, 2)),
+                dma((2, 2)),
                 dma,
-                dma((3,)),
+                dma,
             ],
             compiler_params=pltpu.CompilerParams(
                 collective_id=0, has_side_effects=True, vmem_limit_bytes=56 * 1024 * 1024

time: 86.5 us -> 71.5 us (0.83)
  Pallas kernels: 80.9 us -> 66.3 us
    pallas_call x1, Pallas kernels: 80.9 us -> 66.3 us  [local(): pl.pallas_call(functools.partial(kernel, rows, cols, pairs), out_shape=ja...]
where the time goes in v2:
time: 71.5 us; the launch traced here: 71.1 us
  Pallas kernels  66.3 us (93%)
  local copies, waits for them, and re-layouts  4.79 us (7%)
    pallas_call x1, Pallas kernels, local(): pl.pallas_call(functools.partial(kernel, rows, cols, pairs), out_shape=ja...  66.3 us
    unnamed x1, local copies, waits for them, and re-layouts  4.79 us

profile of v2, /device:TPU:0, one launch (start us, length us, event | category | flops | bytes accessed | tf_op | source)
XLA Modules:
  0.0 71.1 jit_solution(15431558969214123416)
XLA Ops:
  0.0 66.3 %shard_map.28 = f32[1024,1024]{1,0:T(8,128)} custom-call(s32[16]{0:T(128)} %order_ref.1, f32[16,64,1024]{2,1,0:T(8,128)} %bitcast.1), custom_call_target="tpu_custom_call" | custom-call | tf_op jit(solution)/shard_map/pallas_call | solution.py:477
  66.3 4.8 %copy.4 = f32[1024,1024]{1,0:T(8,128)} copy(f32[1024,1024]{1,0:T(8,128)} %shard_map.28) | data formatting | bytes 8388608

commit v3 on v2

--- a/solution.py
+++ b/solution.py
@@ -168,7 +168,6 @@
     core = lax.rem(me, 2)
     chip = lax.div(me, 2)
     partner = me + 1 - 2 * core
-    base = lax.rem(me, pairs)
     has_left = position > 0
     has_right = position < cols - 1
     has = (has_left, has_right)
@@ -192,13 +191,17 @@
 
     lax.fori_loop(0, rows, greet, 0)
 
-    def fill(slot, carry):
-        source = lax.rem(order_ref[slot], 2 * pairs)
-        x0[pl.ds(pl.multiple_of(slot * BLOCK + PAIR, BLOCK), BLOCK), :] = raw[source]
-        return carry
+    def fill(pair):
+        for slot in (2 * pair, 2 * pair + 1):
+            source = lax.rem(order_ref[slot], 2 * pairs)
+            x0[pl.ds(pl.multiple_of(slot * BLOCK + PAIR, BLOCK), BLOCK), :] = raw[source]
+
+    def group_at(place):
+        return pairs // 2 - 1 - place, pairs // 2 + place
 
     arrival.wait()
-    lax.fori_loop(0, 2 * pairs, fill, 0)
+    fill(0)
+    fill(last)
     greeted = rows - 1 + rows * (has_left.astype(jnp.int32) + has_right.astype(jnp.int32))
     pl.semaphore_wait(barrier, greeted)
 
@@ -279,21 +282,28 @@
             total = total + jnp.where(source == me, 0.0, parts[source])
         turns[me] = turn_packed(total)
 
-    def step(index, now):
-        after = 1 - now
+    def take_grams(place, now):
+        chosen = group_at(place)
+        for pair in chosen:
+            grams[pair] = gram_packed(slot_of(pair + 1, now))
+        for pair in chosen:
+            @pl.when(pair != me)
+            def _(pair=pair):
+                gram_copy(pair).start()
+
+    def first_grams(place, carry):
+        for pair in group_at(place):
+            fill(pair)
+        take_grams(place, 0)
+        return carry
+
+    lax.fori_loop(0, pairs // 2 - 1, first_grams, 0)
+    take_grams(pairs // 2 - 1, 0)
+
+    def step(index):
+        now, after = index % 2, 1 - index % 2
         later = buffers[after]
-
-        def take_grams(group, carry):
-            chosen = (2 * group, 2 * group + 1)
-            for pair in chosen:
-                grams[pair] = gram_packed(slot_of(pair + 1, now))
-            for pair in chosen:
-                @pl.when(pair != me)
-                def _(pair=pair):
-                    gram_copy(pair).start()
-            return carry
-
-        lax.fori_loop(0, pairs // 2, take_grams, 0)
+        ending = index == STEPS - 1
 
         @pl.when(me < pairs)
         def _():
@@ -314,48 +324,47 @@
 
                 lax.fori_loop(0, half, spread_halo, 0)
 
-        @pl.when(index > 1)
-        def _():
-            for side in (0, 1):
-                @pl.when(has[1 - side])
-                def _(side=side):
-                    edge_copy(side, after).wait_send()
-
-        if now == 1:
-            @pl.when(index == 1)
-            def _():
-                for side in (0, 1):
-                    @pl.when(has[1 - side])
-                    def _(side=side):
-                        start_copy(side).wait_send()
-
-        def receive(pair):
+        def settle_gram(pair, carry):
             @pl.when(pair != me)
             def _():
+                gram_copy(pair).wait_send()
+            return carry
+
+        lax.fori_loop(0, pairs, settle_gram, 0)
+
+        for side in (0, 1):
+            @pl.when(has[1 - side])
+            def _(side=side):
+                if index > 1:
+                    edge_copy(side, after).wait_send()
+                if index == 1:
+                    start_copy(side).wait_send()
+
+        def relay(pair):
+            @pl.when(jnp.logical_and(pair != me, lax.rem(pair, 2) == core))
+            def _():
                 pass_copy(pair).wait_recv()
-
-                @pl.when(lax.rem(pair, 2) == core)
-                def _():
-                    pass_copy(pair).start()
-
-        def receive_halo(side):
-            @pl.when(has[side])
-            def _():
-                relay_copy(side, now).wait_recv()
-
-                @pl.when(core == direct[side])
-                def _():
-                    relay_copy(side, now).start()
-
-        def pair_at(place):
-            even = 2 * (place - 1)
-            odd = 2 * (place - pairs // 2) + 1
-            shift = jnp.where(place < 2, place, jnp.where(place <= pairs // 2, even, odd))
-            return jnp.bitwise_xor(base, shift)
-
-        def apply_two(first, second):
-            results = [turned(turns[pair], slot_of(pair + 1, now)) for pair in (first, second)]
-            for pair, result in zip((first, second), results):
+                pass_copy(pair).start()
+
+        def receive_group(place):
+            chosen = group_at(place)
+            for pair in chosen:
+                relay(pair)
+            for pair in chosen:
+                @pl.when(jnp.logical_and(pair != me, lax.rem(pair, 2) != core))
+                def _(pair=pair):
+                    pass_copy(pair).wait_recv()
+
+        def settle_group(place):
+            for pair in group_at(place):
+                @pl.when(jnp.logical_and(pair != me, lax.rem(pair, 2) == core))
+                def _(pair=pair):
+                    pass_copy(pair).wait_send()
+
+        def apply_group(place):
+            chosen = group_at(place)
+            results = [turned(turns[pair], slot_of(pair + 1, now)) for pair in chosen]
+            for pair, result in zip(chosen, results):
                 opening = jnp.logical_and(pair == 0, jnp.logical_not(has_left))
                 closing = jnp.logical_and(pair == last, jnp.logical_not(has_right))
                 top = jnp.where(opening, PAIR, jnp.where(closing, pairs * PAIR + BLOCK, (pair + 2) * PAIR))
@@ -363,69 +372,59 @@
                 later[pl.ds(pl.multiple_of(top, BLOCK), BLOCK), :] = result[:BLOCK]
                 later[pl.ds(pl.multiple_of(bottom, BLOCK), BLOCK), :] = result[BLOCK:]
 
-        receive(pair_at(0))
-        receive(pair_at(1))
-        apply_two(pair_at(0), pair_at(1))
-
-        def receive_direct(place, carry):
-            receive(pair_at(place))
+        def next_grams(place):
+            settle_group(place)
+            if not ending:
+                take_grams(place, after)
+
+        receive_group(0)
+        apply_group(0)
+
+        def apply_next(place, carry):
+            receive_group(place)
+            apply_group(place)
+            next_grams(place - 1)
             return carry
 
-        lax.fori_loop(2, pairs // 2 + 1, receive_direct, 0)
-        for side in (0, 1):
-            @pl.when(core == direct[side])
-            def _(side=side):
-                receive_halo(side)
-
-        def apply_rest(group, carry):
-            for place in (2 * group, 2 * group + 1):
-                @pl.when(place > pairs // 2)
-                def _(place=place):
-                    receive(pair_at(place))
-            apply_two(pair_at(2 * group), pair_at(2 * group + 1))
-            return carry
-
-        lax.fori_loop(1, pairs // 2, apply_rest, 0)
-        for side in (0, 1):
-            @pl.when(core != direct[side])
-            def _(side=side):
-                receive_halo(side)
+        lax.fori_loop(1, pairs // 2, apply_next, 0)
+
+        def receive_halo(side):
+            @pl.when(has[side])
+            def _():
+                relay_copy(side, now).wait_recv()
+
+                @pl.when(core == direct[side])
+                def _():
+                    relay_copy(side, now).start()
+
+        for relayed in (False, True):
+            for side in (0, 1):
+                @pl.when((core != direct[side]) == relayed)
+                def _(side=side):
+                    receive_halo(side)
 
         for side in (0, 1):
             @pl.when(has[side])
             def _(side=side):
-                if now == 0:
-                    @pl.when(index == 0)
-                    def _():
-                        start_copy(side).wait_recv()
-
-                    @pl.when(index > 0)
-                    def _():
-                        edge_copy(side, now).wait_recv()
+                if index == 0:
+                    start_copy(side).wait_recv()
                 else:
                     edge_copy(side, now).wait_recv()
                 rest = turned_half(halos[now, side], slot_of(side * (pairs + 1), now), side)
                 target = PAIR if side == 0 else pairs * PAIR + BLOCK
                 later[pl.ds(target, BLOCK), :] = rest
 
-        @pl.when(index < STEPS - 1)
-        def _():
+        next_grams(pairs // 2 - 1)
+        for side in (0, 1):
+            @pl.when(jnp.logical_and(core == direct[side], has[side]))
+            def _(side=side):
+                relay_copy(side, now).wait_send()
+
+        if not ending:
             for side in (0, 1):
                 @pl.when(has[1 - side])
                 def _(side=side):
                     edge_copy(side, after).start()
-
-        def settle(pair, carry):
-            @pl.when(pair != me)
-            def _():
-                gram_copy(pair).wait_send()
-
-                @pl.when(lax.rem(pair, 2) == core)
-                def _():
-                    pass_copy(pair).wait_send()
-            return carry
-
-        lax.fori_loop(0, pairs, settle, 0)
 
         @pl.when(me < pairs)
         def _():
@@ -444,16 +443,8 @@
 
                 lax.fori_loop(0, half, settle_halo, 0)
 
-            @pl.when(jnp.logical_and(core == direct[side], has[side]))
-            def _(side=side):
-                relay_copy(side, now).wait_send()
-
-    def two_steps(index, carry):
-        step(2 * index, 0)
-        step(2 * index + 1, 1)
-        return carry
-
-    lax.fori_loop(0, STEPS // 2, two_steps, 0)
+    for index in range(STEPS):
+        step(index)
     final = STEPS % 2
     result = pltpu.make_async_copy(buffers[final].at[pl.ds(PAIR, pairs * PAIR)], out_ref, out_sem)
     result.start()

time: 71.5 us -> 74.1 us (1.036)
  the two profiles are of different devices: /device:TPU:0 before, /device:TPU:9 now
where the time goes in v3:
time: 74.1 us; the launch traced here: 73.9 us
  Pallas kernels  69.1 us (93%)
  local copies, waits for them, and re-layouts  4.79 us (6%)
    pallas_call x1, Pallas kernels, local(): pl.pallas_call(functools.partial(kernel, rows, cols, pairs), out_shape=ja...  69.1 us
    unnamed x1, local copies, waits for them, and re-layouts  4.79 us

profile of v3, /device:TPU:9, one launch (start us, length us, event | category | flops | bytes accessed | tf_op | source)
XLA Modules:
  0.0 73.9 jit_solution(6977446154873378687)
XLA Ops:
  0.0 69.1 %shard_map.28 = f32[1024,1024]{1,0:T(8,128)} custom-call(s32[16]{0:T(128)} %order_ref.1, f32[16,64,1024]{2,1,0:T(8,128)} %bitcast.1), custom_call_target="tpu_custom_call" | custom-call | tf_op jit(solution)/shard_map/pallas_call | solution.py:468
  69.1 4.8 %copy.4 = f32[1024,1024]{1,0:T(8,128)} copy(f32[1024,1024]{1,0:T(8,128)} %shard_map.28) | data formatting | bytes 8388608

commit v4 on v3

--- a/solution.py
+++ b/solution.py
@@ -157,12 +157,10 @@
     return apply_turn(matrix[:BLOCK] if side == 0 else matrix[BLOCK:], block)
 
 
-def kernel(rows, cols, pairs, order_ref, columns_ref, out_ref, raw, x0, x1, grams, parts, turns, halos,
+def kernel(rows, cols, pairs, order_ref, columns_ref, x1, turns, halos, x0, grams, parts,
            gram_send, gram_recv, turn_send, turn_recv, pass_send, halo_send, halo_recv, relay_send,
-           start_send, start_recv, edge_send, edge_recv, in_sem, out_sem):
+           start_send, start_recv, edge_send, edge_recv):
     buffers = (x0, x1)
-    arrival = pltpu.make_async_copy(columns_ref, raw, in_sem)
-    arrival.start()
     me = lax.axis_index("row")
     position = lax.axis_index("col")
     core = lax.rem(me, 2)
@@ -194,12 +192,11 @@
     def fill(pair):
         for slot in (2 * pair, 2 * pair + 1):
             source = lax.rem(order_ref[slot], 2 * pairs)
-            x0[pl.ds(pl.multiple_of(slot * BLOCK + PAIR, BLOCK), BLOCK), :] = raw[source]
+            x0[pl.ds(pl.multiple_of(slot * BLOCK + PAIR, BLOCK), BLOCK), :] = columns_ref[source]
 
     def group_at(place):
         return pairs // 2 - 1 - place, pairs // 2 + place
 
-    arrival.wait()
     fill(0)
     fill(last)
     greeted = rows - 1 + rows * (has_left.astype(jnp.int32) + has_right.astype(jnp.int32))
@@ -346,11 +343,12 @@
                 pass_copy(pair).wait_recv()
                 pass_copy(pair).start()
 
+        def relay_group(place):
+            for pair in group_at(place):
+                relay(pair)
+
         def receive_group(place):
-            chosen = group_at(place)
-            for pair in chosen:
-                relay(pair)
-            for pair in chosen:
+            for pair in group_at(place):
                 @pl.when(jnp.logical_and(pair != me, lax.rem(pair, 2) != core))
                 def _(pair=pair):
                     pass_copy(pair).wait_recv()
@@ -374,19 +372,31 @@
 
         def next_grams(place):
             settle_group(place)
-            if not ending:
-                take_grams(place, after)
-
-        receive_group(0)
-        apply_group(0)
+            take_grams(place, after)
+
+        if ending:
+            for place in range(pairs // 2):
+                relay_group(place)
+            for place in range(pairs // 2):
+                receive_group(place)
+        else:
+            for place in range(2):
+                relay_group(place)
+            receive_group(0)
+            apply_group(0)
 
         def apply_next(place, carry):
+            @pl.when(place < pairs // 2 - 1)
+            def _():
+                relay_group(place + 1)
+
             receive_group(place)
             apply_group(place)
             next_grams(place - 1)
             return carry
 
-        lax.fori_loop(1, pairs // 2, apply_next, 0)
+        if not ending:
+            lax.fori_loop(1, pairs // 2, apply_next, 0)
 
         def receive_halo(side):
             @pl.when(has[side])
@@ -410,11 +420,16 @@
                     start_copy(side).wait_recv()
                 else:
                     edge_copy(side, now).wait_recv()
-                rest = turned_half(halos[now, side], slot_of(side * (pairs + 1), now), side)
-                target = PAIR if side == 0 else pairs * PAIR + BLOCK
-                later[pl.ds(target, BLOCK), :] = rest
-
-        next_grams(pairs // 2 - 1)
+                if not ending:
+                    rest = turned_half(halos[now, side], slot_of(side * (pairs + 1), now), side)
+                    target = PAIR if side == 0 else pairs * PAIR + BLOCK
+                    later[pl.ds(target, BLOCK), :] = rest
+
+        if ending:
+            for place in range(pairs // 2):
+                settle_group(place)
+        else:
+            next_grams(pairs // 2 - 1)
         for side in (0, 1):
             @pl.when(jnp.logical_and(core == direct[side], has[side]))
             def _(side=side):
@@ -445,15 +460,65 @@
 
     for index in range(STEPS):
         step(index)
-    final = STEPS % 2
-    result = pltpu.make_async_copy(buffers[final].at[pl.ds(PAIR, pairs * PAIR)], out_ref, out_sem)
-    result.start()
     for side in (0, 1):
         @pl.when(has[1 - side])
         def _(side=side):
-            edge_copy(side, 1 - final).wait_send()
-
-    result.wait()
+            edge_copy(side, (STEPS - 1) % 2).wait_send()
+
+
+def closing_kernel(cols, pairs, x, turns, halos, out_ref, result, out_sem):
+    position = lax.axis_index("col")
+    has = (position > 0, position < cols - 1)
+    last = pairs - 1
+    now = (STEPS - 1) % 2
+
+    def out_copy(place, row):
+        rows = pl.ds(pl.multiple_of(row, BLOCK), BLOCK)
+        return pltpu.make_async_copy(result.at[rows], out_ref.at[rows], out_sem.at[place])
+
+    def slot_of(slot):
+        return x[pl.ds(pl.multiple_of(slot * PAIR, PAIR), PAIR), :]
+
+    def put(row, values):
+        result[pl.ds(pl.multiple_of(row, BLOCK), BLOCK), :] = values
+
+    def inner(place, carry):
+        chosen = (2 * place + 1, 2 * place + 2)
+        results = [turned(turns[pair], slot_of(pair + 1)) for pair in chosen]
+        for pair, both in zip(chosen, results):
+            for part, row in enumerate(((pair + 1) * PAIR, (pair - 1) * PAIR + BLOCK)):
+                put(row, both[part * BLOCK : (part + 1) * BLOCK])
+        for pair in chosen:
+            for part, row in enumerate(((pair + 1) * PAIR, (pair - 1) * PAIR + BLOCK)):
+                out_copy(2 * pair + part, row).start()
+        return carry
+
+    lax.fori_loop(0, (pairs - 2) // 2, inner, 0)
+    results = [turned(turns[pair], slot_of(pair + 1)) for pair in (0, last)]
+    first_top = jnp.where(has[0], PAIR, 0)
+    put(first_top, results[0][:BLOCK])
+    put((last - 1) * PAIR + BLOCK, results[1][BLOCK:])
+    kept = (jnp.where(has[0], pairs * PAIR, PAIR), jnp.where(has[1], pairs * PAIR + BLOCK, last * PAIR + BLOCK))
+    put(kept[0], results[0][BLOCK:])
+    put(kept[1], results[1][:BLOCK])
+    out_copy(0, first_top).start()
+    out_copy(1, (last - 1) * PAIR + BLOCK).start()
+    for side in (0, 1):
+        @pl.when(jnp.logical_not(has[side]))
+        def _(side=side):
+            out_copy(2 * last + side, kept[side]).start()
+
+        @pl.when(has[side])
+        def _(side=side):
+            target = 0 if side == 0 else last * PAIR + BLOCK
+            put(target, turned_half(halos[now, side], slot_of(side * (pairs + 1)), side))
+            out_copy(2 * last + side, target).start()
+
+    def settle(place, carry):
+        out_copy(place, 0).wait()
+        return carry
+
+    lax.fori_loop(0, 2 * pairs, settle, 0)
 
 
 def solution(mesh):
@@ -464,20 +529,21 @@
         pairs = width // PAIR
         assert 4 <= pairs <= rows and rows % pairs == 0 and pairs & (pairs - 1) == 0 and STEPS % 2 == 0
         dma = pltpu.SemaphoreType.DMA
-        buffer = pltpu.VMEM((width + 2 * PAIR, length), jnp.float32)
-        return pl.pallas_call(
+        wide = (width + 2 * PAIR, length)
+        vmem = pl.BlockSpec(memory_space=pltpu.VMEM)
+        state = pl.pallas_call(
             functools.partial(kernel, rows, cols, pairs),
-            out_shape=jax.ShapeDtypeStruct((width, length), jnp.float32),
-            in_specs=[pl.BlockSpec(memory_space=pltpu.SMEM), pl.BlockSpec(memory_space=pl.ANY)],
-            out_specs=pl.BlockSpec(memory_space=pl.ANY),
+            out_shape=[
+                jax.ShapeDtypeStruct(wide, jnp.float32),
+                jax.ShapeDtypeStruct((pairs, BLOCK + 8, PAIR), jnp.float32),
+                jax.ShapeDtypeStruct((2, 2, BLOCK + 8, PAIR), jnp.float32),
+            ],
+            in_specs=[pl.BlockSpec(memory_space=pltpu.SMEM), vmem],
+            out_specs=[vmem, vmem, vmem],
             scratch_shapes=[
-                pltpu.VMEM((2 * pairs, BLOCK, length), jnp.float32),
-                buffer,
-                buffer,
+                pltpu.VMEM(wide, jnp.float32),
                 pltpu.VMEM((pairs, PACKED, PAIR), jnp.float32),
                 pltpu.VMEM((rows, PACKED, PAIR), jnp.float32),
-                pltpu.VMEM((pairs, BLOCK + 8, PAIR), jnp.float32),
-                pltpu.VMEM((2, 2, BLOCK + 8, PAIR), jnp.float32),
                 dma((pairs,)),
                 dma((rows,)),
                 dma((rows // 2,)),
@@ -490,13 +556,19 @@
                 dma((2,)),
                 dma((2, 2)),
                 dma((2, 2)),
-                dma,
-                dma,
             ],
             compiler_params=pltpu.CompilerParams(
-                collective_id=0, has_side_effects=True, vmem_limit_bytes=56 * 1024 * 1024
+                collective_id=0, has_side_effects=True, vmem_limit_bytes=20 * 1024 * 1024
             ),
         )(block_order, columns.reshape(2 * pairs, BLOCK, length))
+        return pl.pallas_call(
+            functools.partial(closing_kernel, cols, pairs),
+            out_shape=jax.ShapeDtypeStruct((width, length), jnp.float32),
+            in_specs=[vmem, vmem, vmem],
+            out_specs=pl.BlockSpec(memory_space=pl.ANY),
+            scratch_shapes=[pltpu.VMEM((width + PAIR, length), jnp.float32), dma((2 * pairs,))],
+            compiler_params=pltpu.CompilerParams(vmem_limit_bytes=20 * 1024 * 1024),
+        )(*state)
 
     placed = (P("col", "row"), P("col"))
     return jax.shard_map(local, mesh=mesh, in_specs=placed, out_specs=P("col", "row"), check_vma=False)

time: 74.1 us -> 67.3 us (0.908)
  the two profiles are of different devices: /device:TPU:9 before, /device:TPU:0 now
where the time goes in v4:
time: 67.3 us; the launch traced here: 66.9 us
  Pallas kernels  64.1 us (95%)
  local copies, waits for them, and re-layouts  2.84 us (4%)
    pallas_call x1, Pallas kernels, local(): pl.pallas_call(functools.partial(kernel, rows, cols, pairs), out_shape=[j...  60.8 us
    pallas_call x1, Pallas kernels, local(): pl.pallas_call(functools.partial(closing_kernel, cols, pairs), out_shape=...  3.28 us
    unnamed x4, local copies, waits for them, and re-layouts  2.84 us

profile of v4, /device:TPU:0, one launch (start us, length us, event | category | flops | bytes accessed | tf_op | source)
XLA Modules:
  0.0 66.9 jit_solution(4577646790024373138)
XLA Ops:
  0.0 0.0 copy-start
  0.0 2.2 %copy-done = f32[1024,1024]{1,0:T(8,128)S(1)} copy-done((f32[1024,1024]{1,0:T(8,128)S(1)}, f32[1024,1024]{1,0:T(8,128)}, u32[]{:S(2)}) %copy-start) | copy-done | bytes 4194328
  2.2 0.0 copy-start.1
  2.2 0.7 copy-done.1
  2.8 60.8 %shard_map.28 = (f32[1280,1024]{1,0:T(8,128)S(1)}, f32[8,72,128]{2,1,0:T(8,128)S(1)}, f32[2,2,72,128]{3,2,1,0:T(8,128)S(1)}) custom-call(s32[16]{0:T(128)S(1)} %copy-done.1, f32[16,64,1024]{2,1,0:T(8,128)S(1)} %bitcast.1), custom_call_target="tpu_custom_call" | custom-call | tf_op jit(solution)/shard_map/pallas_call | solution.py:534
  63.6 3.3 %shard_map.29 = f32[1024,1024]{1,0:T(8,128)} custom-call(f32[1280,1024]{1,0:T(8,128)S(1)} %get-tuple-element.8.x, f32[8,72,128]{2,1,0:T(8,128)S(1)} %get-tuple-element.9.turns, f32[2,2,72,128]{3,2,1,0:T(8,128)S(1)} %get-tuple-element.10.halos), custom_call_target="tpu_custom_call" | custom-call | tf_op jit(solution)/shard_map/pallas_call | solution.py:564
Async XLA Ops:
  0.0 2.2 %copy-start = (f32[1024,1024]{1,0:T(8,128)S(1)}, f32[1024,1024]{1,0:T(8,128)}, u32[]{:S(2)}) copy-start(f32[1024,1024]{1,0:T(8,128)} %param.2) | copy-start | bytes 12582916
  2.2 0.7 copy-start.1

commit v5 on v4

v5 whole, which is shorter than its diff:
```python
import functools

import jax
import jax.numpy as jnp
from jax import lax
from jax.experimental import pallas as pl
from jax.experimental.pallas import tpu as pltpu
from jax.sharding import PartitionSpec as P

BLOCK = 64
PAIR = 2 * BLOCK
STEPS = 4
HALF = BLOCK // 2
PACKED = HALF + 8
UPPER = 1.0 + BLOCK * BLOCK * 0.0905
NN = (((1,), (0,)), ((), ()))
NT = (((1,), (1,)), ((), ()))


def split(a):
    high = a.astype(jnp.bfloat16)
    return high, (a - high.astype(jnp.float32)).astype(jnp.bfloat16)


def split3(a):
    high = a.astype(jnp.bfloat16)
    rest = a - high.astype(jnp.float32)
    middle = rest.astype(jnp.bfloat16)
    return high, middle, (rest - middle.astype(jnp.float32)).astype(jnp.bfloat16)


def product(a, b, dims=NN):
    return lax.dot_general(a, b, dims, preferred_element_type=jnp.float32)


def mm3(a, b, dims=NN):
    (ah, am), (bh, bm) = split(a), split(b)
    count = a.shape[0]
    stacked = product(jnp.concatenate([ah, am], axis=0), bh, dims)
    return stacked[:count] + stacked[count:] + product(ah, bm, dims)


def mm6(a, b, dims=NN):
    (ah, am, al), (bh, bm, bl) = split3(a), split3(b)
    count = a.shape[0]
    first = product(jnp.concatenate([ah, am, al], axis=0), bh, dims)
    second = product(jnp.concatenate([ah, am], axis=0), bm, dims)
    small = first[2 * count :] + second[count:] + product(ah, bl, dims)
    return first[:count] + ((first[count : 2 * count] + second[:count]) + small)


def left(a):
    return a[:, :BLOCK]


def inverse(system, eye):
    low = 2.0 / (1.0 + UPPER)
    y = system * low
    reach = low * (2.0 - low)
    scale = 2.0 / (1.0 + reach)
    x = (scale * low) * (2.0 * eye - y)
    y = scale * (2.0 * y - mm3(left(y), y))
    low = scale * reach
    while low < 0.999:
        reach = low * (2.0 - low)
        scale = 2.0 / (1.0 + reach)
        following = scale * (2.0 * y - mm3(left(y), y))
        x = scale * (2.0 * x - mm3(left(x), y))
        y = following
        low = scale * reach
    return x


def coupling_packed(total):
    row = lax.broadcasted_iota(jnp.int32, (HALF, PAIR), 0)
    lane = lax.broadcasted_iota(jnp.int32, (HALF, PAIR), 1)
    cross = total[:HALF]
    norms = total[HALF : HALF + 1]
    bottom_norms = total[HALF + 1 : HALF + 2]
    upper_norms = jnp.sum(jnp.where(lane == row, norms, 0.0), axis=1, keepdims=True)
    lower_norms = jnp.sum(jnp.where(lane == row + HALF, norms, 0.0), axis=1, keepdims=True)
    top_norms = jnp.where(lane < BLOCK, upper_norms, lower_norms)
    spread = bottom_norms - top_norms
    square = spread * spread + 4.0 * cross * cross
    radius = jnp.sqrt(square)
    scale_term = (top_norms + bottom_norms) / BLOCK
    return 2.0 * cross * spread / (square + jnp.abs(spread) * radius + scale_term * scale_term)


def doubled(packed):
    lane = lax.broadcasted_iota(jnp.int32, (HALF, PAIR), 1)
    rolled = pltpu.roll(packed, BLOCK, 1)
    return jnp.concatenate([jnp.where(lane < BLOCK, packed, rolled), jnp.where(lane < BLOCK, rolled, packed)], axis=0)


def inverse_packed(packed):
    coupling = doubled(packed)
    rows = lax.broadcasted_iota(jnp.int32, (BLOCK, PAIR), 0)
    lanes = lax.broadcasted_iota(jnp.int32, (BLOCK, PAIR), 1)
    columns = jnp.where(lanes < BLOCK, lanes, lanes - BLOCK)
    eye = jnp.where(rows == columns, 1.0, 0.0).astype(jnp.float32)
    narrow = left(coupling)
    narrow_t = narrow.T
    system = eye + mm3(narrow, jnp.concatenate([narrow, narrow], axis=0), NT)
    x = inverse(system, eye)
    residual = eye - x - mm6(narrow, mm6(narrow_t, x))
    x = x + mm3(left(x), residual)
    return jnp.where(lanes[:HALF] < BLOCK, x[:HALF], x[HALF:])


def lefts_of(matrix):
    lane = lax.broadcasted_iota(jnp.int32, (BLOCK, PAIR), 1)
    high = matrix.astype(jnp.bfloat16).astype(jnp.float32)
    rest = matrix - high
    middle = rest.astype(jnp.bfloat16).astype(jnp.float32)
    first = jnp.where(lane < BLOCK, high, middle)
    second = jnp.where(lane < BLOCK, rest - middle, high)
    return jnp.concatenate([first, second], axis=1).astype(jnp.bfloat16)


def rights_of(block):
    high, low = split(block)
    return jnp.concatenate([high, high, high, low], axis=0)


def opened(packed, block):
    coupling = doubled(packed)
    flipped = jnp.concatenate([coupling, coupling], axis=0).T[:BLOCK]
    return block[:BLOCK] - product(lefts_of(coupling), rights_of(block[BLOCK:])), lefts_of(flipped)


def upper_solved(packed, rest):
    return product(lefts_of(doubled(packed)), rights_of(rest))


def lower_solved(flip, upper, block):
    return block[BLOCK:] + product(flip, rights_of(upper))


def turned(packed, rest, flip, block):
    upper = upper_solved(packed, rest)
    return 2.0 * upper - block[:BLOCK], 2.0 * lower_solved(flip, upper, block) - block[BLOCK:]


def turned_half(packed, rest, flip, block, side):
    upper = upper_solved(packed, rest)
    if side == 0:
        return 2.0 * upper - block[:BLOCK]
    return 2.0 * lower_solved(flip, upper, block) - block[BLOCK:]


def gram_packed(block):
    high, low = split(block)
    lefts = jnp.concatenate([high[:BLOCK], low[:BLOCK]], axis=0)
    rights = jnp.concatenate([high[BLOCK:], low[BLOCK:]], axis=0)
    parts = product(lefts, rights, NT)
    halves = parts[:BLOCK] + parts[BLOCK:]
    cross = halves + pltpu.roll(halves, BLOCK, 1)
    lane = lax.broadcasted_iota(jnp.int32, (HALF, PAIR), 1)
    cross = jnp.where(lane < BLOCK, cross[:HALF], cross[HALF:])
    squares = block * block
    partial = squares[:, :128]
    for start in range(128, squares.shape[1], 128):
        partial = partial + squares[:, start : start + 128]
    norms = jnp.broadcast_to(jnp.sum(partial.T, axis=0, keepdims=True), (8, PAIR))
    rows = lax.broadcasted_iota(jnp.int32, (8, PAIR), 0)
    lanes = lax.broadcasted_iota(jnp.int32, (8, PAIR), 1)
    norms = jnp.where(jnp.logical_and(rows == 1, lanes < BLOCK), pltpu.roll(norms, BLOCK, 1), norms)
    return jnp.concatenate([cross, norms], axis=0)


def kernel(rows, cols, pairs, order_ref, columns_ref, x1, couplings, inverses, halo_couplings, halo_inverses,
           x0, grams, parts, rests, flips, gram_send, gram_recv, coupling_send, coupling_recv, inverse_send,
           inverse_recv, halo_send, halo_recv, start_send, start_recv, edge_send, edge_recv):
    buffers = (x0, x1)
    me = lax.axis_index("row")
    position = lax.axis_index("col")
    partner = jnp.bitwise_xor(me, 1)
    has_left = position > 0
    has_right = position < cols - 1
    has = (has_left, has_right)
    beside = (position - 1, position + 1)
    last = pairs - 1
    kinds = ((couplings, halo_couplings, coupling_send, coupling_recv), (inverses, halo_inverses, inverse_send, inverse_recv))

    barrier = pltpu.get_barrier_semaphore()

    def greet(other, carry):
        @pl.when(other != me)
        def _():
            pl.semaphore_signal(barrier, inc=1, device_id={"row": other})

        for side in (0, 1):
            @pl.when(has[side])
            def _(side=side):
                pl.semaphore_signal(barrier, inc=1, device_id={"row": other, "col": beside[side]})
        return carry

    lax.fori_loop(0, rows, greet, 0)

    def fill(pair):
        for slot in (2 * pair, 2 * pair + 1):
            source = lax.rem(order_ref[slot], 2 * pairs)
            x0[pl.ds(pl.multiple_of(slot * BLOCK + PAIR, BLOCK), BLOCK), :] = columns_ref[source]

    def group_at(place):
        return pairs // 2 - 1 - place, pairs // 2 + place

    fill(0)
    fill(last)
    greeted = rows - 1 + rows * (has_left.astype(jnp.int32) + has_right.astype(jnp.int32))
    pl.semaphore_wait(barrier, greeted)

    def gram_copy(pair):
        return pltpu.make_async_remote_copy(
            src_ref=grams.at[pair], dst_ref=parts.at[me], send_sem=gram_send.at[pair], recv_sem=gram_recv.at[me],
            device_id={"row": pair},
        )

    def gram_arrival(source):
        return pltpu.make_async_remote_copy(
            src_ref=parts.at[source], dst_ref=parts.at[source], send_sem=gram_send.at[0],
            recv_sem=gram_recv.at[source], device_id={"row": partner},
        )

    def spread_copy(kind, other):
        values, _, send, recv = kinds[kind]
        return pltpu.make_async_remote_copy(
            src_ref=values.at[me], dst_ref=values.at[me], send_sem=send.at[other], recv_sem=recv.at[me],
            device_id={"row": jnp.bitwise_xor(me, other)},
        )

    def spread_arrival(kind, pair):
        values, _, send, recv = kinds[kind]
        return pltpu.make_async_remote_copy(
            src_ref=values.at[pair], dst_ref=values.at[pair], send_sem=send.at[0], recv_sem=recv.at[pair],
            device_id={"row": partner},
        )

    def halo_copy(kind, other, side, now):
        values, halo, _, _ = kinds[kind]
        return pltpu.make_async_remote_copy(
            src_ref=values.at[me], dst_ref=halo.at[now, side], send_sem=halo_send.at[kind, other],
            recv_sem=halo_recv.at[kind, now, side],
            device_id={"row": jnp.bitwise_xor(me, other), "col": beside[1 - side]},
        )

    def halo_arrival(kind, side, now):
        halo = kinds[kind][1]
        return pltpu.make_async_remote_copy(
            src_ref=halo.at[now, side], dst_ref=halo.at[now, side], send_sem=halo_send.at[kind, 0],
            recv_sem=halo_recv.at[kind, now, side], device_id={"row": partner},
        )

    far = (pairs + 1) * PAIR

    def start_copy(side):
        source = pairs * PAIR if side == 0 else PAIR
        target = 0 if side == 0 else far
        return pltpu.make_async_remote_copy(
            src_ref=x0.at[pl.ds(source, PAIR)], dst_ref=x0.at[pl.ds(target, PAIR)], send_sem=start_send.at[side],
            recv_sem=start_recv.at[side], device_id={"col": beside[1 - side]},
        )

    def edge_copy(side, after):
        source = pairs * PAIR if side == 0 else PAIR + BLOCK
        target = 0 if side == 0 else far + BLOCK
        return pltpu.make_async_remote_copy(
            src_ref=buffers[after].at[pl.ds(source, BLOCK)], dst_ref=buffers[after].at[pl.ds(target, BLOCK)],
            send_sem=edge_send.at[after, side], recv_sem=edge_recv.at[after, side],
            device_id={"col": beside[1 - side]},
        )

    for side in (0, 1):
        @pl.when(has[1 - side])
        def _(side=side):
            start_copy(side).start()

    def slot_of(slot, now):
        return buffers[now][pl.ds(pl.multiple_of(slot * PAIR, PAIR), PAIR), :]

    def spread(kind, now):
        def spread_out(place, carry):
            spread_copy(kind, rows - place).start()
            return carry

        lax.fori_loop(1, rows, spread_out, 0)
        for side, owner in ((0, last), (1, 0)):
            @pl.when(jnp.logical_and(me == owner, has[1 - side]))
            def _(side=side):
                def spread_halo(place, carry):
                    halo_copy(kind, rows - place, side, now).start()
                    return carry

                lax.fori_loop(1, rows + 1, spread_halo, 0)

    def settle_spread(kind, now):
        def settle_out(other, carry):
            spread_copy(kind, other).wait_send()
            return carry

        lax.fori_loop(1, rows, settle_out, 0)
        for side, owner in ((0, last), (1, 0)):
            @pl.when(jnp.logical_and(me == owner, has[1 - side]))
            def _(side=side):
                def settle_halo(other, carry):
                    halo_copy(kind, other, side, now).wait_send()
                    return carry

                lax.fori_loop(0, rows, settle_halo, 0)

    def own(now):
        def gather(source, carry):
            @pl.when(source != me)
            def _():
                gram_arrival(source).wait_recv()
            return carry

        lax.fori_loop(0, rows, gather, 0)
        total = grams[me]
        for source in range(rows):
            total = total + jnp.where(source == me, 0.0, parts[source])
        couplings[me] = coupling_packed(total)
        spread(0, now)
        inverses[me] = inverse_packed(couplings[me])
        spread(1, now)

    def take_grams(place, now):
        chosen = group_at(place)
        for pair in chosen:
            grams[pair] = gram_packed(slot_of(pair + 1, now))
        for pair in chosen:
            @pl.when(pair != me)
            def _(pair=pair):
                gram_copy(pair).start()

    def first_grams(place, carry):
        for pair in group_at(place):
            fill(pair)
        take_grams(place, 0)
        return carry

    lax.fori_loop(0, pairs // 2 - 1, first_grams, 0)
    take_grams(pairs // 2 - 1, 0)

    def step(index):
        now, after = index % 2, 1 - index % 2
        later = buffers[after]
        ending = index == STEPS - 1

        @pl.when(me < pairs)
        def _():
            own(now)

        def settle_gram(pair, carry):
            @pl.when(pair != me)
            def _():
                gram_copy(pair).wait_send()
            return carry

        lax.fori_loop(0, pairs, settle_gram, 0)

        for side in (0, 1):
            @pl.when(has[1 - side])
            def _(side=side):
                if index > 1:
                    edge_copy(side, after).wait_send()
                if index == 1:
                    start_copy(side).wait_send()

        def receive(kind, place):
            for pair in group_at(place):
                @pl.when(pair != me)
                def _(pair=pair):
                    spread_arrival(kind, pair).wait_recv()

        def receive_halo(kind, side):
            halo_arrival(kind, side, now).wait_recv()
            if kind == 0:
                if index == 0:
                    start_copy(side).wait_recv()
                else:
                    edge_copy(side, now).wait_recv()

        def open_group(place):
            receive(0, place)
            for pair in group_at(place):
                rests[pair + 1], flips[pair + 1] = opened(couplings[pair], slot_of(pair + 1, now))

        def close_group(place):
            receive(1, place)
            chosen = group_at(place)
            results = [turned(inverses[pair], rests[pair + 1], flips[pair + 1], slot_of(pair + 1, now)) for pair in chosen]
            for pair, (upper, lower) in zip(chosen, results):
                opening = jnp.logical_and(pair == 0, jnp.logical_not(has_left))
                closing = jnp.logical_and(pair == last, jnp.logical_not(has_right))
                top = jnp.where(opening, PAIR, jnp.where(closing, pairs * PAIR + BLOCK, (pair + 2) * PAIR))
                bottom = jnp.where(opening, 2 * PAIR, pair * PAIR + BLOCK)
                later[pl.ds(pl.multiple_of(top, BLOCK), BLOCK), :] = upper
                later[pl.ds(pl.multiple_of(bottom, BLOCK), BLOCK), :] = lower

        if ending:
            for kind in (0, 1):
                for place in range(pairs // 2):
                    receive(kind, place)
                for side in (0, 1):
                    @pl.when(has[side])
                    def _(kind=kind, side=side):
                        receive_halo(kind, side)
        else:
            open_group(0)
            open_group(1)
            close_group(0)

            def close_next(place, carry):
                @pl.when(place < pairs // 2 - 1)
                def _():
                    open_group(place + 1)

                close_group(place)
                take_grams(place - 1, after)
                return carry

            lax.fori_loop(1, pairs // 2, close_next, 0)
            for side in (0, 1):
                @pl.when(has[side])
                def _(side=side):
                    slot = side * (pairs + 1)
                    receive_halo(0, side)
                    rests[slot], flips[slot] = opened(halo_couplings[now, side], slot_of(slot, now))

            for side in (0, 1):
                @pl.when(has[side])
                def _(side=side):
                    slot = side * (pairs + 1)
                    receive_halo(1, side)
                    target = PAIR if side == 0 else pairs * PAIR + BLOCK
                    later[pl.ds(target, BLOCK), :] = turned_half(
                        halo_inverses[now, side], rests[slot], flips[slot], slot_of(slot, now), side
                    )

            take_grams(pairs // 2 - 1, after)
            for side in (0, 1):
                @pl.when(has[1 - side])
                def _(side=side):
                    edge_copy(side, after).start()

        @pl.when(me < pairs)
        def _():
            for kind in (0, 1):
                settle_spread(kind, now)

    for index in range(STEPS):
        step(index)
    for side in (0, 1):
        @pl.when(has[1 - side])
        def _(side=side):
            edge_copy(side, (STEPS - 1) % 2).wait_send()


def closing_kernel(cols, pairs, x, couplings, inverses, halo_couplings, halo_inverses, out_ref, result, out_sem):
    position = lax.axis_index("col")
    has = (position > 0, position < cols - 1)
    last = pairs - 1
    now = (STEPS - 1) % 2

    def out_copy(place, row):
        rows = pl.ds(pl.multiple_of(row, BLOCK), BLOCK)
        return pltpu.make_async_copy(result.at[rows], out_ref.at[rows], out_sem.at[place])

    def slot_of(slot):
        return x[pl.ds(pl.multiple_of(slot * PAIR, PAIR), PAIR), :]

    def put(row, values):
        result[pl.ds(pl.multiple_of(row, BLOCK), BLOCK), :] = values

    def finished(pair):
        block = slot_of(pair + 1)
        return turned(inverses[pair], *opened(couplings[pair], block), block)

    def finished_half(side):
        block = slot_of(side * (pairs + 1))
        return turned_half(halo_inverses[now, side], *opened(halo_couplings[now, side], block), block, side)

    def inner(place, carry):
        chosen = (2 * place + 1, 2 * place + 2)
        results = [finished(pair) for pair in chosen]
        for pair, both in zip(chosen, results):
            for part, row in enumerate(((pair + 1) * PAIR, (pair - 1) * PAIR + BLOCK)):
                put(row, both[part])
        for pair in chosen:
            for part, row in enumerate(((pair + 1) * PAIR, (pair - 1) * PAIR + BLOCK)):
                out_copy(2 * pair + part, row).start()
        return carry

    lax.fori_loop(0, (pairs - 2) // 2, inner, 0)
    results = [finished(pair) for pair in (0, last)]
    first_top = jnp.where(has[0], PAIR, 0)
    put(first_top, results[0][0])
    put((last - 1) * PAIR + BLOCK, results[1][1])
    kept = (jnp.where(has[0], pairs * PAIR, PAIR), jnp.where(has[1], pairs * PAIR + BLOCK, last * PAIR + BLOCK))
    put(kept[0], results[0][1])
    put(kept[1], results[1][0])
    out_copy(0, first_top).start()
    out_copy(1, (last - 1) * PAIR + BLOCK).start()
    for side in (0, 1):
        @pl.when(jnp.logical_not(has[side]))
        def _(side=side):
            out_copy(2 * last + side, kept[side]).start()

        @pl.when(has[side])
        def _(side=side):
            target = 0 if side == 0 else last * PAIR + BLOCK
            put(target, finished_half(side))
            out_copy(2 * last + side, target).start()

    def settle(place, carry):
        out_copy(place, 0).wait()
        return carry

    lax.fori_loop(0, 2 * pairs, settle, 0)


def solution(mesh):
    rows, cols = mesh.shape["row"], mesh.shape["col"]

    def local(columns, block_order):
        width, length = columns.shape
        pairs = width // PAIR
        assert 4 <= pairs <= rows and rows % pairs == 0 and rows & (rows - 1) == 0 and STEPS % 2 == 0
        dma = pltpu.SemaphoreType.DMA
        wide = (width + 2 * PAIR, length)
        vmem = pl.BlockSpec(memory_space=pltpu.VMEM)
        state = pl.pallas_call(
            functools.partial(kernel, rows, cols, pairs),
            out_shape=[
                jax.ShapeDtypeStruct(wide, jnp.float32),
                jax.ShapeDtypeStruct((pairs, HALF, PAIR), jnp.float32),
                jax.ShapeDtypeStruct((pairs, HALF, PAIR), jnp.float32),
                jax.ShapeDtypeStruct((2, 2, HALF, PAIR), jnp.float32),
                jax.ShapeDtypeStruct((2, 2, HALF, PAIR), jnp.float32),
            ],
            in_specs=[pl.BlockSpec(memory_space=pltpu.SMEM), vmem],
            out_specs=[vmem] * 5,
            scratch_shapes=[
                pltpu.VMEM(wide, jnp.float32),
                pltpu.VMEM((pairs, PACKED, PAIR), jnp.float32),
                pltpu.VMEM((rows, PACKED, PAIR), jnp.float32),
                pltpu.VMEM((pairs + 2, BLOCK, length), jnp.float32),
                pltpu.VMEM((pairs + 2, BLOCK, 2 * PAIR), jnp.bfloat16),
                dma((pairs,)),
                dma((rows,)),
                dma((rows,)),
                dma((pairs,)),
                dma((rows,)),
                dma((pairs,)),
                dma((2, rows)),
                dma((2, 2, 2)),
                dma((2,)),
                dma((2,)),
                dma((2, 2)),
                dma((2, 2)),
            ],
            compiler_params=pltpu.CompilerParams(
                collective_id=0, has_side_effects=True, vmem_limit_bytes=20 * 1024 * 1024
            ),
        )(block_order, columns.reshape(2 * pairs, BLOCK, length))
        return pl.pallas_call(
            functools.partial(closing_kernel, cols, pairs),
            out_shape=jax.ShapeDtypeStruct((width, length), jnp.float32),
            in_specs=[vmem] * 5,
            out_specs=pl.BlockSpec(memory_space=pl.ANY),
            scratch_shapes=[pltpu.VMEM((width + PAIR, length), jnp.float32), dma((2 * pairs,))],
            compiler_params=pltpu.CompilerParams(vmem_limit_bytes=20 * 1024 * 1024),
        )(*state)

    placed = (P("col", "row"), P("col"))
    return jax.shard_map(local, mesh=mesh, in_specs=placed, out_specs=P("col", "row"), check_vma=False)
```

time: 67.3 us -> 67.1 us (level)
    pallas_call x1, Pallas kernels: 3.28 us -> 5.61 us  [local(): pl.pallas_call(functools.partial(closing_kernel, cols, pairs), out_shape=...]
    pallas_call x1, Pallas kernels: 60.8 us -> 58.5 us  [local(): pl.pallas_call(functools.partial(kernel, rows, cols, pairs), out_shape=[j...]
where the time goes in v5:
time: 67.1 us; the launch traced here: 67 us
  Pallas kernels  64.1 us (96%)
  local copies, waits for them, and re-layouts  2.84 us (4%)
    pallas_call x1, Pallas kernels, local(): pl.pallas_call(functools.partial(kernel, rows, cols, pairs), out_shape=[j...  58.5 us
    pallas_call x1, Pallas kernels, local(): pl.pallas_call(functools.partial(closing_kernel, cols, pairs), out_shape=...  5.61 us
    unnamed x4, local copies, waits for them, and re-layouts  2.84 us

profile of v5, /device:TPU:0, one launch (start us, length us, event | category | flops | bytes accessed | tf_op | source)
XLA Modules:
  0.0 67.0 jit_solution(6396659550270127461)
XLA Ops:
  0.0 0.0 copy-start
  0.0 2.2 %copy-done = f32[1024,1024]{1,0:T(8,128)S(1)} copy-done((f32[1024,1024]{1,0:T(8,128)S(1)}, f32[1024,1024]{1,0:T(8,128)}, u32[]{:S(2)}) %copy-start) | copy-done | bytes 4194328
  2.2 0.0 copy-start.1
  2.2 0.7 copy-done.1
  2.8 58.5 %shard_map.28 = (f32[1280,1024]{1,0:T(8,128)S(1)}, f32[8,32,128]{2,1,0:T(8,128)S(1)}, f32[8,32,128]{2,1,0:T(8,128)S(1)}, f32[2,2,32,128]{3,2,1,0:T(8,128)S(1)}, f32[2,2,32,128]{3,2,1,0:T(8,128)S(1)}) custom-call(s32[16]{0:T(128)S(1)} %copy-done.1, f32[16,64,1024]{2,1,0:T(8,128)S(1)} %bitcast.1), custom_call_target="tpu_custom_call" | custom-call | tf_op jit(solution)/shard_map/pallas_call | solution.py:534
  61.4 5.6 %shard_map.29 = f32[1024,1024]{1,0:T(8,128)} custom-call(f32[1280,1024]{1,0:T(8,128)S(1)} %get-tuple-element.10.x, f32[8,32,128]{2,1,0:T(8,128)S(1)} %get-tuple-element.11.couplings, f32[8,32,128]{2,1,0:T(8,128)S(1)} %get-tuple-element.12.inverses, f32[2,2,32,128]{3,2,1,0:T(8,128)S(1)} %get-tuple-element.13.halo_couplings, ...), custom_call_target="tpu_custom_call" | custom-call | tf_op jit(solution)/shard_map/pallas_call | solution.py:568
Async XLA Ops:
  0.0 2.2 %copy-start = (f32[1024,1024]{1,0:T(8,128)S(1)}, f32[1024,1024]{1,0:T(8,128)}, u32[]{:S(2)}) copy-start(f32[1024,1024]{1,0:T(8,128)} %param.2) | copy-start | bytes 12582916
  2.2 0.7 copy-start.1

commit v6 on v5

--- a/solution.py
+++ b/solution.py
@@ -126,11 +126,13 @@
 def opened(packed, block):
     coupling = doubled(packed)
     flipped = jnp.concatenate([coupling, coupling], axis=0).T[:BLOCK]
-    return block[:BLOCK] - product(lefts_of(coupling), rights_of(block[BLOCK:])), lefts_of(flipped)
+    rest = block[:BLOCK] - product(lefts_of(coupling), rights_of(block[BLOCK:]))
+    return jnp.concatenate(split(rest), axis=0), lefts_of(flipped)
 
 
 def upper_solved(packed, rest):
-    return product(lefts_of(doubled(packed)), rights_of(rest))
+    high = rest[:BLOCK]
+    return product(lefts_of(doubled(packed)), jnp.concatenate([high, high, rest], axis=0))
 
 
 def lower_solved(flip, upper, block):
@@ -169,8 +171,8 @@
     return jnp.concatenate([cross, norms], axis=0)
 
 
-def kernel(rows, cols, pairs, order_ref, columns_ref, x1, couplings, inverses, halo_couplings, halo_inverses,
-           x0, grams, parts, rests, flips, gram_send, gram_recv, coupling_send, coupling_recv, inverse_send,
+def kernel(rows, cols, pairs, order_ref, columns_ref, x1, inverses, halo_inverses, rests, flips,
+           couplings, halo_couplings, x0, grams, parts, gram_send, gram_recv, coupling_send, coupling_recv, inverse_send,
            inverse_recv, halo_send, halo_recv, start_send, start_recv, edge_send, edge_recv):
     buffers = (x0, x1)
     me = lax.axis_index("row")
@@ -213,13 +215,13 @@
 
     def gram_copy(pair):
         return pltpu.make_async_remote_copy(
-            src_ref=grams.at[pair], dst_ref=parts.at[me], send_sem=gram_send.at[pair], recv_sem=gram_recv.at[me],
+            src_ref=grams.at[pair, pl.ds(0, HALF + 2)], dst_ref=parts.at[me, pl.ds(0, HALF + 2)], send_sem=gram_send.at[pair], recv_sem=gram_recv.at[me],
             device_id={"row": pair},
         )
 
     def gram_arrival(source):
         return pltpu.make_async_remote_copy(
-            src_ref=parts.at[source], dst_ref=parts.at[source], send_sem=gram_send.at[0],
+            src_ref=parts.at[source, pl.ds(0, HALF + 2)], dst_ref=parts.at[source, pl.ds(0, HALF + 2)], send_sem=gram_send.at[0],
             recv_sem=gram_recv.at[source], device_id={"row": partner},
         )
 
@@ -384,8 +386,9 @@
 
         def open_group(place):
             receive(0, place)
-            for pair in group_at(place):
-                rests[pair + 1], flips[pair + 1] = opened(couplings[pair], slot_of(pair + 1, now))
+            made = [opened(couplings[pair], slot_of(pair + 1, now)) for pair in group_at(place)]
+            for pair, (rest, flip) in zip(group_at(place), made):
+                rests[pair + 1], flips[pair + 1] = rest, flip
 
         def close_group(place):
             receive(1, place)
@@ -399,52 +402,58 @@
                 later[pl.ds(pl.multiple_of(top, BLOCK), BLOCK), :] = upper
                 later[pl.ds(pl.multiple_of(bottom, BLOCK), BLOCK), :] = lower
 
+        def receive_halos(kind):
+            for side in (0, 1):
+                @pl.when(has[side])
+                def _(side=side):
+                    receive_halo(kind, side)
+
+        def open_halos():
+            receive_halos(0)
+            made = [opened(halo_couplings[now, side], slot_of(side * (pairs + 1), now)) for side in (0, 1)]
+            for side in (0, 1):
+                rests[side * (pairs + 1)], flips[side * (pairs + 1)] = made[side]
+
+        def close_halos():
+            receive_halos(1)
+            slots = (0, pairs + 1)
+            made = [
+                turned_half(halo_inverses[now, side], rests[slots[side]], flips[slots[side]], slot_of(slots[side], now), side)
+                for side in (0, 1)
+            ]
+            targets = (jnp.where(has_left, PAIR, 0), jnp.where(has_right, pairs * PAIR + BLOCK, far + BLOCK))
+            for side in (0, 1):
+                later[pl.ds(pl.multiple_of(targets[side], BLOCK), BLOCK), :] = made[side]
+
         if ending:
-            for kind in (0, 1):
-                for place in range(pairs // 2):
-                    receive(kind, place)
-                for side in (0, 1):
-                    @pl.when(has[side])
-                    def _(kind=kind, side=side):
-                        receive_halo(kind, side)
+            for place in range(pairs // 2):
+                open_group(place)
+            open_halos()
+            for place in range(pairs // 2):
+                receive(1, place)
+            receive_halos(1)
         else:
             open_group(0)
             open_group(1)
             close_group(0)
 
             def close_next(place, carry):
-                @pl.when(place < pairs // 2 - 1)
-                def _():
-                    open_group(place + 1)
-
+                open_group(place + 1)
                 close_group(place)
                 take_grams(place - 1, after)
                 return carry
 
-            lax.fori_loop(1, pairs // 2, close_next, 0)
-            for side in (0, 1):
-                @pl.when(has[side])
-                def _(side=side):
-                    slot = side * (pairs + 1)
-                    receive_halo(0, side)
-                    rests[slot], flips[slot] = opened(halo_couplings[now, side], slot_of(slot, now))
-
-            for side in (0, 1):
-                @pl.when(has[side])
-                def _(side=side):
-                    slot = side * (pairs + 1)
-                    receive_halo(1, side)
-                    target = PAIR if side == 0 else pairs * PAIR + BLOCK
-                    later[pl.ds(target, BLOCK), :] = turned_half(
-                        halo_inverses[now, side], rests[slot], flips[slot], slot_of(slot, now), side
-                    )
-
-            take_grams(pairs // 2 - 1, after)
+            lax.fori_loop(1, pairs // 2 - 1, close_next, 0)
+            open_halos()
             for side in (0, 1):
                 @pl.when(has[1 - side])
                 def _(side=side):
                     edge_copy(side, after).start()
 
+            close_group(pairs // 2 - 1)
+            take_grams(pairs // 2 - 2, after)
+            close_halos()
+            take_grams(pairs // 2 - 1, after)
         @pl.when(me < pairs)
         def _():
             for kind in (0, 1):
@@ -458,7 +467,7 @@
             edge_copy(side, (STEPS - 1) % 2).wait_send()
 
 
-def closing_kernel(cols, pairs, x, couplings, inverses, halo_couplings, halo_inverses, out_ref, result, out_sem):
+def closing_kernel(cols, pairs, x, inverses, halo_inverses, rests, flips, out_ref, result, out_sem):
     position = lax.axis_index("col")
     has = (position > 0, position < cols - 1)
     last = pairs - 1
@@ -475,44 +484,47 @@
         result[pl.ds(pl.multiple_of(row, BLOCK), BLOCK), :] = values
 
     def finished(pair):
-        block = slot_of(pair + 1)
-        return turned(inverses[pair], *opened(couplings[pair], block), block)
+        return turned(inverses[pair], rests[pair + 1], flips[pair + 1], slot_of(pair + 1))
 
     def finished_half(side):
-        block = slot_of(side * (pairs + 1))
-        return turned_half(halo_inverses[now, side], *opened(halo_couplings[now, side], block), block, side)
-
-    def inner(place, carry):
-        chosen = (2 * place + 1, 2 * place + 2)
+        slot = side * (pairs + 1)
+        return turned_half(halo_inverses[now, side], rests[slot], flips[slot], slot_of(slot), side)
+
+    spare = (pairs * PAIR, pairs * PAIR + BLOCK)
+    given = (0, last * PAIR + BLOCK)
+    halfway = pairs // 2
+
+    def inner(chosen):
         results = [finished(pair) for pair in chosen]
-        for pair, both in zip(chosen, results):
-            for part, row in enumerate(((pair + 1) * PAIR, (pair - 1) * PAIR + BLOCK)):
-                put(row, both[part])
+        for pair, (upper, lower) in zip(chosen, results):
+            put((pair + 1) * PAIR, upper)
+            put((pair - 1) * PAIR + BLOCK, lower)
+
+    def send_inner(chosen):
         for pair in chosen:
-            for part, row in enumerate(((pair + 1) * PAIR, (pair - 1) * PAIR + BLOCK)):
-                out_copy(2 * pair + part, row).start()
-        return carry
-
-    lax.fori_loop(0, (pairs - 2) // 2, inner, 0)
+            out_copy(2 * pair, (pair + 1) * PAIR).start()
+            out_copy(2 * pair + 1, (pair - 1) * PAIR + BLOCK).start()
+
+    sets = (tuple(range(1, halfway + 1)), tuple(range(halfway + 1, last)))
+    inner(sets[0])
+    send_inner(sets[0])
+    inner(sets[1])
+    first_top = jnp.where(has[0], PAIR, 0)
+    lowest = (last - 1) * PAIR + BLOCK
+    kept = (jnp.where(has[0], spare[0], PAIR), jnp.where(has[1], spare[1], last * PAIR + BLOCK))
     results = [finished(pair) for pair in (0, last)]
-    first_top = jnp.where(has[0], PAIR, 0)
+    halves = [finished_half(side) for side in (0, 1)]
     put(first_top, results[0][0])
-    put((last - 1) * PAIR + BLOCK, results[1][1])
-    kept = (jnp.where(has[0], pairs * PAIR, PAIR), jnp.where(has[1], pairs * PAIR + BLOCK, last * PAIR + BLOCK))
+    put(lowest, results[1][1])
     put(kept[0], results[0][1])
     put(kept[1], results[1][0])
+    for side in (0, 1):
+        put(jnp.where(has[side], given[side], spare[side]), halves[side])
+    send_inner(sets[1])
     out_copy(0, first_top).start()
-    out_copy(1, (last - 1) * PAIR + BLOCK).start()
+    out_copy(1, lowest).start()
     for side in (0, 1):
-        @pl.when(jnp.logical_not(has[side]))
-        def _(side=side):
-            out_copy(2 * last + side, kept[side]).start()
-
-        @pl.when(has[side])
-        def _(side=side):
-            target = 0 if side == 0 else last * PAIR + BLOCK
-            put(target, finished_half(side))
-            out_copy(2 * last + side, target).start()
+        out_copy(2 * last + side, jnp.where(has[side], given[side], kept[side])).start()
 
     def settle(place, carry):
         out_copy(place, 0).wait()
@@ -536,18 +548,18 @@
             out_shape=[
                 jax.ShapeDtypeStruct(wide, jnp.float32),
                 jax.ShapeDtypeStruct((pairs, HALF, PAIR), jnp.float32),
-                jax.ShapeDtypeStruct((pairs, HALF, PAIR), jnp.float32),
                 jax.ShapeDtypeStruct((2, 2, HALF, PAIR), jnp.float32),
-                jax.ShapeDtypeStruct((2, 2, HALF, PAIR), jnp.float32),
+                jax.ShapeDtypeStruct((pairs + 2, 2 * BLOCK, length), jnp.bfloat16),
+                jax.ShapeDtypeStruct((pairs + 2, BLOCK, 2 * PAIR), jnp.bfloat16),
             ],
             in_specs=[pl.BlockSpec(memory_space=pltpu.SMEM), vmem],
             out_specs=[vmem] * 5,
             scratch_shapes=[
+                pltpu.VMEM((pairs, HALF, PAIR), jnp.float32),
+                pltpu.VMEM((2, 2, HALF, PAIR), jnp.float32),
                 pltpu.VMEM(wide, jnp.float32),
                 pltpu.VMEM((pairs, PACKED, PAIR), jnp.float32),
                 pltpu.VMEM((rows, PACKED, PAIR), jnp.float32),
-                pltpu.VMEM((pairs + 2, BLOCK, length), jnp.float32),
-                pltpu.VMEM((pairs + 2, BLOCK, 2 * PAIR), jnp.bfloat16),
                 dma((pairs,)),
                 dma((rows,)),
                 dma((rows,)),

time: 67.1 us -> 66.1 us (0.985)
  Pallas kernels: 64.1 us -> 62.9 us
    pallas_call x1, Pallas kernels: 5.61 us -> 4.06 us  [local(): pl.pallas_call(functools.partial(closing_kernel, cols, pairs), out_shape=...]
where the time goes in v6:
time: 66.1 us; the launch traced here: 65.9 us
  Pallas kernels  62.9 us (95%)
  local copies, waits for them, and re-layouts  2.84 us (4%)
    pallas_call x1, Pallas kernels, local(): pl.pallas_call(functools.partial(kernel, rows, cols, pairs), out_shape=[j...  58.8 us
    pallas_call x1, Pallas kernels, local(): pl.pallas_call(functools.partial(closing_kernel, cols, pairs), out_shape=...  4.06 us
    unnamed x4, local copies, waits for them, and re-layouts  2.84 us

profile of v6, /device:TPU:0, one launch (start us, length us, event | category | flops | bytes accessed | tf_op | source)
XLA Modules:
  0.0 65.9 jit_solution(14843326742607230561)
XLA Ops:
  0.0 0.0 copy-start
  0.0 2.2 %copy-done = f32[1024,1024]{1,0:T(8,128)S(1)} copy-done((f32[1024,1024]{1,0:T(8,128)S(1)}, f32[1024,1024]{1,0:T(8,128)}, u32[]{:S(2)}) %copy-start) | copy-done | bytes 4194328
  2.2 0.0 copy-start.1
  2.2 0.7 copy-done.1
  2.8 58.8 %shard_map.28 = (f32[1280,1024]{1,0:T(8,128)S(1)}, f32[8,32,128]{2,1,0:T(8,128)S(1)}, f32[2,2,32,128]{3,2,1,0:T(8,128)S(1)}, bf16[10,128,1024]{2,1,0:T(8,128)(2,1)S(1)}, bf16[10,64,256]{2,1,0:T(8,128)(2,1)S(1)}) custom-call(s32[16]{0:T(128)S(1)} %copy-done.1, f32[16,64,1024]{2,1,0:T(8,128)S(1)} %bitcast.1), custom_call_target="tpu_custom_call" | custom-call | tf_op jit(solution)/shard_map/pallas_call | solution.py:546
  61.7 4.1 %shard_map.29 = f32[1024,1024]{1,0:T(8,128)} custom-call(f32[1280,1024]{1,0:T(8,128)S(1)} %get-tuple-element.10.x, f32[8,32,128]{2,1,0:T(8,128)S(1)} %get-tuple-element.11.inverses, f32[2,2,32,128]{3,2,1,0:T(8,128)S(1)} %get-tuple-element.12.halo_inverses, bf16[10,128,1024]{2,1,0:T(8,128)(2,1)S(1)} %get-tuple-element.13.rests, ...), custom_call_target="tpu_custom_call" | custom-call | tf_op jit(solution)/shard_map/pallas_call | solution.py:580
Async XLA Ops:
  0.0 2.2 %copy-start = (f32[1024,1024]{1,0:T(8,128)S(1)}, f32[1024,1024]{1,0:T(8,128)}, u32[]{:S(2)}) copy-start(f32[1024,1024]{1,0:T(8,128)} %param.2) | copy-start | bytes 12582916
  2.2 0.7 copy-start.1

commit v7 on v6

--- a/solution.py
+++ b/solution.py
@@ -256,12 +256,16 @@
 
     far = (pairs + 1) * PAIR
 
-    def start_copy(side):
+    parts_of = ((0, PAIR - HALF), (PAIR - HALF, HALF))
+
+    def start_copy(side, part):
+        first, count = parts_of[part]
         source = pairs * PAIR if side == 0 else PAIR
         target = 0 if side == 0 else far
         return pltpu.make_async_remote_copy(
-            src_ref=x0.at[pl.ds(source, PAIR)], dst_ref=x0.at[pl.ds(target, PAIR)], send_sem=start_send.at[side],
-            recv_sem=start_recv.at[side], device_id={"col": beside[1 - side]},
+            src_ref=x0.at[pl.ds(source + first, count)], dst_ref=x0.at[pl.ds(target + first, count)],
+            send_sem=start_send.at[part, side], recv_sem=start_recv.at[part, side],
+            device_id={"col": beside[1 - side]},
         )
 
     def edge_copy(side, after):
@@ -276,7 +280,7 @@
     for side in (0, 1):
         @pl.when(has[1 - side])
         def _(side=side):
-            start_copy(side).start()
+            start_copy(side, 0).start()
 
     def slot_of(slot, now):
         return buffers[now][pl.ds(pl.multiple_of(slot * PAIR, PAIR), PAIR), :]
@@ -354,6 +358,12 @@
         def _():
             own(now)
 
+        if index == 0:
+            for side in (0, 1):
+                @pl.when(has[1 - side])
+                def _(side=side):
+                    start_copy(side, 1).start()
+
         def settle_gram(pair, carry):
             @pl.when(pair != me)
             def _():
@@ -368,7 +378,8 @@
                 if index > 1:
                     edge_copy(side, after).wait_send()
                 if index == 1:
-                    start_copy(side).wait_send()
+                    start_copy(side, 0).wait_send()
+                    start_copy(side, 1).wait_send()
 
         def receive(kind, place):
             for pair in group_at(place):
@@ -380,7 +391,8 @@
             halo_arrival(kind, side, now).wait_recv()
             if kind == 0:
                 if index == 0:
-                    start_copy(side).wait_recv()
+                    start_copy(side, 0).wait_recv()
+                    start_copy(side, 1).wait_recv()
                 else:
                     edge_copy(side, now).wait_recv()
 
@@ -568,8 +580,8 @@
                 dma((pairs,)),
                 dma((2, rows)),
                 dma((2, 2, 2)),
-                dma((2,)),
-                dma((2,)),
+                dma((2, 2)),
+                dma((2, 2)),
                 dma((2, 2)),
                 dma((2, 2)),
             ],

time: 66.1 us -> 67.7 us (1.024)
  Pallas kernels: 62.9 us -> 64.5 us
    pallas_call x1, Pallas kernels: 58.8 us -> 60.4 us  [local(): pl.pallas_call(functools.partial(kernel, rows, cols, pairs), out_shape=[j...]
where the time goes in v7:
time: 67.7 us; the launch traced here: 67.5 us
  Pallas kernels  64.5 us (95%)
  local copies, waits for them, and re-layouts  2.84 us (4%)
    pallas_call x1, Pallas kernels, local(): pl.pallas_call(functools.partial(kernel, rows, cols, pairs), out_shape=[j...  60.4 us
    pallas_call x1, Pallas kernels, local(): pl.pallas_call(functools.partial(closing_kernel, cols, pairs), out_shape=...  4.06 us
    unnamed x4, local copies, waits for them, and re-layouts  2.84 us

profile of v7, /device:TPU:0, one launch (start us, length us, event | category | flops | bytes accessed | tf_op | source)
XLA Modules:
  0.0 67.5 jit_solution(11905050697148426639)
XLA Ops:
  0.0 0.0 copy-start
  0.0 2.2 %copy-done = f32[1024,1024]{1,0:T(8,128)S(1)} copy-done((f32[1024,1024]{1,0:T(8,128)S(1)}, f32[1024,1024]{1,0:T(8,128)}, u32[]{:S(2)}) %copy-start) | copy-done | bytes 4194328
  2.2 0.0 copy-start.1
  2.2 0.7 copy-done.1
  2.8 60.4 %shard_map.28 = (f32[1280,1024]{1,0:T(8,128)S(1)}, f32[8,32,128]{2,1,0:T(8,128)S(1)}, f32[2,2,32,128]{3,2,1,0:T(8,128)S(1)}, bf16[10,128,1024]{2,1,0:T(8,128)(2,1)S(1)}, bf16[10,64,256]{2,1,0:T(8,128)(2,1)S(1)}) custom-call(s32[16]{0:T(128)S(1)} %copy-done.1, f32[16,64,1024]{2,1,0:T(8,128)S(1)} %bitcast.1), custom_call_target="tpu_custom_call" | custom-call | tf_op jit(solution)/shard_map/pallas_call | solution.py:558
  63.3 4.1 %shard_map.29 = f32[1024,1024]{1,0:T(8,128)} custom-call(f32[1280,1024]{1,0:T(8,128)S(1)} %get-tuple-element.10.x, f32[8,32,128]{2,1,0:T(8,128)S(1)} %get-tuple-element.11.inverses, f32[2,2,32,128]{3,2,1,0:T(8,128)S(1)} %get-tuple-element.12.halo_inverses, bf16[10,128,1024]{2,1,0:T(8,128)(2,1)S(1)} %get-tuple-element.13.rests, ...), custom_call_target="tpu_custom_call" | custom-call | tf_op jit(solution)/shard_map/pallas_call | solution.py:592
Async XLA Ops:
  0.0 2.2 %copy-start = (f32[1024,1024]{1,0:T(8,128)S(1)}, f32[1024,1024]{1,0:T(8,128)}, u32[]{:S(2)}) copy-start(f32[1024,1024]{1,0:T(8,128)} %param.2) | copy-start | bytes 12582916
  2.2 0.7 copy-start.1
